TPU v7x, 16 devices: a 4x2x1 block of a 4x4x8 slice. The times are simulated.
16 devices in a mesh: rep: 2 (over y, z), dp: 8 (over x, core).
Axes of the slice: x: 4, y: 2, z: 1, core: 2. Of those that a mesh axis runs over, the one named last changes fastest.
The devices are a block of a 4x4x8 slice.
Arguments:
- x: bfloat16 [16, 2048, 896], P(('rep', 'dp')), parts along dimension 0
- dy: bfloat16 [16, 2048, 896], P(('rep', 'dp')), parts along dimension 0
- w_gate: bfloat16 [2, 896, 2304], replicated
- w_up: bfloat16 [2, 896, 2304], replicated
- w_down: bfloat16 [2, 2304, 896], replicated
- m_w_gate: float32 [2, 896, 2304], P(None, 'dp')
- m_w_up: float32 [2, 896, 2304], P(None, 'dp')
- m_w_down: float32 [2, 2304, 896], P(None, 'dp')
- v_w_gate: float32 [2, 896, 2304], P(None, 'dp')
- v_w_up: float32 [2, 896, 2304], P(None, 'dp')
- v_w_down: float32 [2, 2304, 896], P(None, 'dp')
Outputs:
- output 1: bfloat16 [4, 896, 2304], P('rep'), parts along dimension 0
- output 2: bfloat16 [4, 896, 2304], P('rep'), parts along dimension 0
- output 3: bfloat16 [4, 2304, 896], P('rep'), parts along dimension 0
- output 4: float32 [4, 896, 2304], P('rep', 'dp'), parts along dimension 0
- output 5: float32 [4, 896, 2304], P('rep', 'dp'), parts along dimension 0
- output 6: float32 [4, 2304, 896], P('rep', 'dp'), parts along dimension 0
- output 7: float32 [4, 896, 2304], P('rep', 'dp'), parts along dimension 0
- output 8: float32 [4, 896, 2304], P('rep', 'dp'), parts along dimension 0
- output 9: float32 [4, 2304, 896], P('rep', 'dp'), parts along dimension 0
There are 2 independent parts. A program takes and returns all parts, laid end to end along the dimension named above; an argument that names none is the same for every part.
All inputs are finite; a program needn't handle non-finite values.
Results may differ from a plain program's by a relative error of at most 0.022.
Values are sent between devices in bfloat16 or wider.
A program may use at most 768 MiB of HBM per device.

v0:
```python
import jax
import jax.numpy as jnp
from jax import lax

NAMES = ("w_gate", "w_up", "w_down")


def matmul(a, w):
    return jnp.dot(a, w, preferred_element_type=jnp.float32).astype(jnp.bfloat16)


def normed(h):
    wide = h.astype(jnp.float32)
    scale = lax.rsqrt(jnp.mean(wide**2, -1, keepdims=True) + 1e-6)
    return (wide * scale).astype(jnp.bfloat16)


def layer(h, w):
    a = normed(h)
    gate = jnp.dot(a, w["w_gate"], preferred_element_type=jnp.float32)
    up = jnp.dot(a, w["w_up"], preferred_element_type=jnp.float32)
    return h + matmul((jax.nn.silu(gate) * up).astype(jnp.bfloat16), w["w_down"])


def adamw(w, m, v, g):
    m = 0.9 * m + 0.1 * g
    v = 0.95 * v + 0.05 * g * g
    step = m * lax.rsqrt(v + 1e-8) + 0.1 * w
    return (w - 0.02 * step).astype(jnp.bfloat16), m, v


def clipped(gradients, sum_of_squares, count):
    factor = jnp.minimum(1.0, 0.5 * lax.rsqrt(sum_of_squares / count + 1e-30))
    return [g * factor for g in gradients]


def stack(weights, h):
    for number in range(weights["w_gate"].shape[0]):
        h = layer(h, {name: w[number] for name, w in weights.items()})
    return h


def solution(mesh):
    groups = mesh.shape["rep"]

    def step(x, dy, *arrays):
        weights, m, v = (arrays[i : i + 3] for i in (0, 3, 6))
        x, dy = (t.reshape(groups, -1, *t.shape[1:]) for t in (x, dy))

        def of_a_group(x, dy):
            _, back = jax.vjp(lambda w: stack(w, x), dict(zip(NAMES, weights, strict=True)))
            by_weights = back(dy)[0]
            gradients = [by_weights[name].astype(jnp.float32) for name in NAMES]
            gradients = clipped(gradients, sum(jnp.sum(g * g) for g in gradients), sum(g.size for g in gradients))
            new = [adamw(w.astype(jnp.float32), m, v, g) for w, m, v, g in zip(weights, m, v, gradients, strict=True)]
            return tuple(one[which] for which in range(3) for one in new)

        return tuple(t.reshape(-1, *t.shape[2:]) for t in jax.vmap(of_a_group)(x, dy))

    return step
```

profile of v0, /device:TPU:113, one launch (start us, length us, event | category | flops | bytes accessed | tf_op | source)
XLA Modules:
  0.0 696.9 jit_solution(11755756593146932353)
XLA Ops:
  10.1 6.1 copy
  16.2 13.7 %fusion.65 = f32[2048,2304]{1,0:T(8,128)S(1)} fusion(bf16[2,896,2304]{2,1,0:T(8,128)(2,1)} %param, bf16[1,2048,896]{2,1,0:T(8,128)(2,1)} %param.2, f32[2048]{0:T(1024)S(1)} %add_rsqrt_fusion), kind=kOutput, calls=%fused_computation.77 | convolution fusion | flops 8461221888 | bytes 26681344 | tf_op jit(solution)/vmap(jvp())/dot_general | solution.py:20
  29.9 18.8 %fusion.63 = f32[2048,2304]{1,0:T(8,128)} fusion(bf16[2,896,2304]{2,1,0:T(8,128)(2,1)} %param.3, bf16[1,2048,896]{2,1,0:T(8,128)(2,1)S(1)} %copy-done.1, f32[2048]{0:T(1024)S(1)} %add_rsqrt_fusion), kind=kOutput, calls=%fused_computation.75 | convolution fusion | flops 8461221888 | bytes 26681344 | tf_op jit(solution)/vmap(jvp())/dot_general | solution.py:21
  48.7 14.1 %fusion.28 = bf16[2048,2304]{1,0:T(8,128)(2,1)} fusion(f32[2048,2304]{1,0:T(8,128)} %fusion.63, f32[2048,2304]{1,0:T(8,128)S(1)} %fusion.65), kind=kLoop, calls=%fused_computation.43 | loop fusion | flops 28311552 | bytes 47185920
  62.7 13.2 %fusion.37 = (f32[2048]{0:T(1024)S(1)}, bf16[1,1,2048,896]{2,3,1,0:T(8,128)(2,1)S(1)}) fusion(bf16[2048,2304]{1,0:T(8,128)(2,1)} %fusion.28, bf16[2,2304,896]{2,1,0:T(8,128)(2,1)} %param.4, bf16[1,2048,896]{1,2,0:T(8,128)(2,1)S(1)} %copy-done.4), kind=kOutput, calls=%fused_computation.54 | convolution fusion | flops 8464889856 | bytes 20914176 | tf_op jit(solution)/vmap(jvp())/dot_general | solution.py:9
  76.0 16.4 %fusion.52 = f32[2048,2304]{1,0:T(8,128)} fusion(bf16[2,896,2304]{2,1,0:T(8,128)(2,1)} %param, bf16[1,1,2048,896]{2,3,1,0:T(8,128)(2,1)S(1)} %get-tuple-element.10, f32[2048]{0:T(1024)S(1)} %bitcast.326), kind=kOutput, calls=%fused_computation.64 | convolution fusion | flops 8461221888 | bytes 26681344 | tf_op jit(solution)/vmap(jvp())/dot_general | solution.py:20
  92.4 15.2 %fusion.56 = f32[2048,2304]{1,0:T(8,128)} fusion(bf16[2,896,2304]{2,1,0:T(8,128)(2,1)} %param.3, bf16[1,1,2048,896]{2,3,1,0:T(8,128)(2,1)S(1)} %get-tuple-element.10, f32[2048]{0:T(1024)S(1)} %bitcast.327), kind=kOutput, calls=%fused_computation.68 | convolution fusion | flops 8461221888 | bytes 26681344 | tf_op jit(solution)/vmap(jvp())/dot_general | solution.py:21
  107.6 12.6 %fusion.26 = bf16[1,1,2048,2304]{3,2,1,0:T(8,128)(2,1)} fusion(bf16[2,2304,896]{2,1,0:T(8,128)(2,1)S(1)} %bitcast.322, bf16[1,2048,896]{2,1,0:T(8,128)(2,1)S(1)} %copy-done.3), kind=kOutput, calls=%fused_computation.41 | convolution fusion | flops 8460435456 | bytes 17235968 | tf_op jit(solution)/vmap(transpose(jvp()))/dot_general | solution.py:9
  120.2 6.0 copy.1
  126.2 16.3 %fusion.6 = bf16[2048,2304]{1,0:T(8,128)(2,1)S(1)} fusion(f32[2048,2304]{1,0:T(8,128)} %fusion.52, f32[2048,2304]{1,0:T(8,128)} %fusion.56, bf16[1,1,2048,2304]{3,2,1,0:T(8,128)(2,1)} %fusion.26), kind=kLoop, calls=%fused_computation.11 | loop fusion | flops 56623104 | bytes 56623104
  146.2 11.7 %fusion.54 = bf16[2048,896]{0,1:T(8,128)(2,1)} fusion(bf16[2048,2304]{1,0:T(8,128)(2,1)S(1)} %fusion.6, bf16[2,896,2304]{2,1,0:T(8,128)(2,1)} %param), kind=kOutput, calls=%fused_computation.66 | convolution fusion | flops 8455716864 | bytes 17235968 | tf_op jit(solution)/vmap(transpose(jvp()))/dot_general | solution.py:20
  158.0 21.1 %fusion.39 = (f32[2048]{0:T(1024)S(1)}, bf16[2048,896]{0,1:T(8,128)(2,1)}) fusion(bf16[1,1,2048,896]{2,3,1,0:T(8,128)(2,1)} %copy-done.6, bf16[2048,896]{0,1:T(8,128)(2,1)} %fusion.54, bf16[2,896,2304]{2,1,0:T(8,128)(2,1)} %param.3, bf16[1,1,2048,2304]{3,2,1,0:T(8,128)(2,1)} %fusion.26, f32[2048,2304]{1,0:T(8,128)} %fusion.52), kind=kOutput, calls=%fused_computation.56 | convolution fusion | flops 8495036416 | bytes 43458560 | tf_op jit(solution)/vmap(transpose(jvp()))/dot_general | solution.py:21
  179.1 6.9 fusion.73
  187.8 15.0 %convolution_bitcast_fusion = f32[1,2304,896]{2,1,0:T(8,128)} fusion(bf16[2048,2304]{1,0:T(8,128)(2,1)} %fusion.28, bf16[2048,896]{0,1:T(8,128)(2,1)S(1)} %fusion.73), kind=kOutput, calls=%fused_computation.62 | convolution fusion | flops 8455716864 | bytes 21364736 | tf_op jit(solution)/vmap(transpose(jvp()))/dot_general | solution.py:9
  203.0 20.0 %fusion.40 = f32[1,2304,896]{2,1,0:T(8,128)} fusion(f32[2048,2304]{1,0:T(8,128)} %fusion.56, f32[2048,2304]{1,0:T(8,128)} %fusion.52, bf16[1,2048,896]{2,1,0:T(8,128)(2,1)} %param.5), kind=kOutput, calls=%fused_computation.58 | convolution fusion | flops 8484028416 | bytes 49676288 | tf_op jit(solution)/vmap(transpose(jvp()))/dot_general | solution.py:9
  223.2 15.4 %fusion.27 = bf16[1,1,2048,2304]{3,2,1,0:T(8,128)(2,1)} fusion(bf16[2048,896]{0,1:T(8,128)(2,1)} %copy-done.7, bf16[2,2304,896]{2,1,0:T(8,128)(2,1)} %param.4), kind=kOutput, calls=%fused_computation.42 | convolution fusion | flops 8460435456 | bytes 17235968 | tf_op jit(solution)/vmap(transpose(jvp()))/dot_general | solution.py:9
  238.6 17.6 %fusion.49 = f32[1,896,2304]{2,1,0:T(8,128)} fusion(bf16[1,1,2048,2304]{3,2,1,0:T(8,128)(2,1)} %fusion.27, f32[2048,2304]{1,0:T(8,128)} %copy-done, bf16[1,2048,896]{1,2,0:T(8,128)(2,1)S(1)} %copy-done.5, f32[2048]{0:T(1024)S(1)} %copy-done.9), kind=kOutput, calls=%fused_computation.61 | convolution fusion | flops 8489533440 | bytes 40247296 | tf_op jit(solution)/vmap(transpose(jvp()))/dot_general | solution.py:21
  256.3 18.9 %fusion.43 = f32[1,896,2304]{2,1,0:T(8,128)} fusion(bf16[1,1,2048,2304]{3,2,1,0:T(8,128)(2,1)} %fusion.26, f32[2048,2304]{1,0:T(8,128)} %fusion.52, bf16[1,1,2048,896]{2,3,1,0:T(8,128)(2,1)} %copy-done.6, f32[2048]{0:T(1024)S(1)} %bitcast.329), kind=kOutput, calls=%fused_computation.59 | convolution fusion | flops 8489533440 | bytes 40247296 | tf_op jit(solution)/vmap(transpose(jvp()))/dot_general | solution.py:21
  275.4 24.9 %fusion.46 = f32[1,896,2304]{2,1,0:T(8,128)} fusion(f32[2048,2304]{1,0:T(8,128)} %copy-done, f32[2048,2304]{1,0:T(8,128)} %fusion.63, bf16[1,1,2048,2304]{3,2,1,0:T(8,128)(2,1)} %fusion.27, bf16[1,2048,896]{1,2,0:T(8,128)(2,1)} %copy, f32[2048]{0:T(1024)S(1)} %copy-done.9), kind=kOutput, calls=%fused_computation.60 | convolution fusion | flops 8513126400 | bytes 59121664 | tf_op jit(solution)/vmap(transpose(jvp()))/dot_general | solution.py:20
  300.4 15.4 %convolution_bitcast_fusion.1 = f32[1,896,2304]{2,1,0:T(8,128)} fusion(bf16[2048,2304]{1,0:T(8,128)(2,1)} %copy-done.2, bf16[1,1,2048,896]{2,3,1,0:T(8,128)(2,1)} %copy-done.6, f32[2048]{0:T(1024)S(1)} %bitcast.330), kind=kOutput, calls=%fused_computation.63 | convolution fusion | flops 8461221888 | bytes 21372928 | tf_op jit(solution)/vmap(transpose(jvp()))/dot_general | solution.py:20
  321.4 32.1 %reduce-scatter.25.cloned.1.call-done = f32[1,112,2304]{2,1,0:T(8,128)} async-done(((f32[1,896,2304]{2,1,0:T(8,128)}), f32[1,112,2304]{2,1,0:T(8,128)}) %reduce-scatter.25.cloned.1.call-update) | async-done | bytes 1032208
  354.8 48.4 %reduce-scatter.23.cloned.1.call-done = f32[1,112,2304]{2,1,0:T(8,128)} async-done(((f32[1,896,2304]{2,1,0:T(8,128)}), f32[1,112,2304]{2,1,0:T(8,128)}) %reduce-scatter.23.cloned.1.call-update) | async-done | bytes 1032208
  405.6 47.8 %reduce-scatter.21.cloned.1.call-done = f32[1,112,2304]{2,1,0:T(8,128)} async-done(((f32[1,896,2304]{2,1,0:T(8,128)}), f32[1,112,2304]{2,1,0:T(8,128)}) %reduce-scatter.21.cloned.1.call-update) | async-done | bytes 1032208
  454.7 49.0 %reduce-scatter.19.cloned.1.call-done = f32[1,112,2304]{2,1,0:T(8,128)} async-done(((f32[1,896,2304]{2,1,0:T(8,128)}), f32[1,112,2304]{2,1,0:T(8,128)}) %reduce-scatter.19.cloned.1.call-update) | async-done | bytes 1032208
  508.1 14.0 %all-reduce.16 = f32[1]{0:T(128)} all-reduce(f32[1]{0:T(128)} %bitcast.50), channel_id=5, replica_groups=mesh['rep'=2,'dp'=8] {'dp'}, use_global_device_ids=true, to_apply=%region_3.4.clone | all-reduce | flops 1 | bytes 8 | tf_op jit(solution)/vmap()/reduce_sum | solution.py:54
  522.8 6.0 fusion.127
  541.1 32.5 %all-gather.14.cloned.1.call-done = bf16[1,2,2304,896]{3,2,1,0:T(8,128)(2,1)} async-done(((bf16[1,2,288,896]{3,2,1,0:T(8,128)(2,1)}), bf16[1,2,2304,896]{3,2,1,0:T(8,128)(2,1)}) %all-gather.14.cloned.1.call-update) | async-done | bytes 8257552 | tf_op jit(solution)/reshape | solution.py:58
  573.5 47.3 %all-gather.12.cloned.1.call-done = bf16[1,2,896,2304]{3,2,1,0:T(8,128)(2,1)} async-done(((bf16[1,2,112,2304]{3,2,1,0:T(8,128)(2,1)}), bf16[1,2,896,2304]{3,2,1,0:T(8,128)(2,1)}) %all-gather.12.cloned.1.call-update) | async-done | bytes 8257552 | tf_op jit(solution)/reshape | solution.py:58
  620.8 47.3 %all-gather.10.cloned.1.call-done = bf16[1,2,896,2304]{3,2,1,0:T(8,128)(2,1)} async-done(((bf16[1,2,112,2304]{3,2,1,0:T(8,128)(2,1)}), bf16[1,2,896,2304]{3,2,1,0:T(8,128)(2,1)}) %all-gather.10.cloned.1.call-update) | async-done | bytes 8257552 | tf_op jit(solution)/reshape | solution.py:58
  668.1 7.2 %copy.5 = bf16[2,896,2304]{2,1,0:T(8,128)(2,1)} copy(bf16[2,896,2304]{2,1,0:T(8,128)(2,1)} %bitcast.320) | data formatting | bytes 16515072
  675.3 7.2 %copy.6 = bf16[2,896,2304]{2,1,0:T(8,128)(2,1)} copy(bf16[2,896,2304]{2,1,0:T(8,128)(2,1)} %bitcast.319) | data formatting | bytes 16515072
  682.5 7.3 %copy.7 = bf16[2,2304,896]{2,1,0:T(8,128)(2,1)} copy(bf16[2,2304,896]{2,1,0:T(8,128)(2,1)} %bitcast.318) | data formatting | bytes 16515072
  (64 shorter events, 33.6 us)
Async XLA Ops:
  7.2 310.5 %reduce-scatter.29.cloned.1.call-start = ((), (), s32[]{:S(2)}) async-start(), calls=%async_computation.14 | async-start | bytes 9289728
  16.1 13.7 %copy-start.8 = (f32[2048]{0:T(1024)}, f32[2048]{0:T(1024)S(1)}, u32[]{:S(2)}) copy-start(f32[2048]{0:T(1024)S(1)} %add_rsqrt_fusion) | copy-start | bytes 24580
  16.1 13.7 %copy-start.1 = (bf16[1,2048,896]{2,1,0:T(8,128)(2,1)S(1)}, bf16[1,2048,896]{2,1,0:T(8,128)(2,1)}, u32[]{:S(2)}) copy-start(bf16[1,2048,896]{2,1,0:T(8,128)(2,1)} %param.2) | copy-start | bytes 11010052
  29.9 18.8 %copy-start = (f32[2048,2304]{1,0:T(8,128)}, f32[2048,2304]{1,0:T(8,128)S(1)}, u32[]{:S(2)}) copy-start(f32[2048,2304]{1,0:T(8,128)S(1)} %fusion.65) | copy-start | bytes 56623108
  48.7 14.1 %copy-start.4 = (bf16[1,2048,896]{1,2,0:T(8,128)(2,1)S(1)}, bf16[1,2048,896]{1,2,0:T(8,128)(2,1)}, u32[]{:S(2)}) copy-start(bf16[1,2048,896]{1,2,0:T(8,128)(2,1)} %copy) | copy-start | bytes 11010052
  76.0 16.4 %copy-start.6 = (bf16[1,1,2048,896]{2,3,1,0:T(8,128)(2,1)}, bf16[1,1,2048,896]{2,3,1,0:T(8,128)(2,1)S(1)}, u32[]{:S(2)}) copy-start(bf16[1,1,2048,896]{2,3,1,0:T(8,128)(2,1)S(1)} %get-tuple-element.10) | copy-start | bytes 11010052
  76.0 31.6 %slice-start = ((s8[8257536]{0:T(1024)(128)(4,1)}), s8[4194304]{0:T(1024)(128)(4,1)S(1)}, s32[]{:S(2)}) async-start(s8[8257536]{0:T(1024)(128)(4,1)} %bitcast.321), calls=%async_computation.15 | async-start | bytes 8388608
  92.4 15.2 %copy-start.3 = (bf16[1,2048,896]{2,1,0:T(8,128)(2,1)S(1)}, bf16[1,2048,896]{2,1,0:T(8,128)(2,1)}, u32[]{:S(2)}) copy-start(bf16[1,2048,896]{2,1,0:T(8,128)(2,1)} %param.5) | copy-start | bytes 11010052
  92.4 15.2 %slice-start.1 = ((s8[8257536]{0:T(1024)(128)(4,1)}), s8[4063232]{0:T(1024)(128)(4,1)S(1)}, s32[]{:S(2)}) async-start(s8[8257536]{0:T(1024)(128)(4,1)} %bitcast.321), calls=%async_computation.16 | async-start | bytes 8126464
  142.6 3.7 copy-start.2
  186.0 1.8 copy-start.7
  202.9 116.1 %reduce-scatter.27.cloned.1.call-start = ((), (), s32[]{:S(2)}) async-start(), calls=%async_computation.13 | async-start | bytes 9289728
  223.1 15.5 %copy-start.9 = (f32[2048]{0:T(1024)S(1)}, f32[2048]{0:T(1024)}, u32[]{:S(2)}) copy-start(f32[2048]{0:T(1024)} %copy-done.8) | copy-start | bytes 24580
  223.1 130.4 %reduce-scatter.25.cloned.1.call-start = ((), (), s32[]{:S(2)}) async-start(), calls=%async_computation.12 | async-start | bytes 9289728
  223.2 15.4 %copy-start.5 = (bf16[1,2048,896]{1,2,0:T(8,128)(2,1)S(1)}, bf16[1,2048,896]{1,2,0:T(8,128)(2,1)}, u32[]{:S(2)}) copy-start(bf16[1,2048,896]{1,2,0:T(8,128)(2,1)} %copy) | copy-start | bytes 11010052
  256.3 146.9 %reduce-scatter.23.cloned.1.call-start = ((), (), s32[]{:S(2)}) async-start(), calls=%async_computation.11 | async-start | bytes 9289728
  275.3 178.2 %reduce-scatter.21.cloned.1.call-start = ((), (), s32[]{:S(2)}) async-start(), calls=%async_computation.10 | async-start | bytes 9289728
  300.3 203.4 %reduce-scatter.19.cloned.1.call-start = ((), (), s32[]{:S(2)}) async-start(), calls=%async_computation.9 | async-start | bytes 9289728
  315.8 0.7 copy-start.10
  315.8 257.7 %all-gather.14.cloned.1.call-start = ((), (), s32[]{:S(2)}) async-start(), calls=%async_computation.8 | async-start | bytes 9289728 | tf_op jit(solution)/reshape | solution.py:58
  528.9 92.0 %all-gather.12.cloned.1.call-start = ((), (), s32[]{:S(2)}) async-start(), calls=%async_computation.7 | async-start | bytes 9289728 | tf_op jit(solution)/reshape | solution.py:58
  535.0 133.1 %all-gather.10.cloned.1.call-start = ((), (), s32[]{:S(2)}) async-start(), calls=%async_computation.6 | async-start | bytes 9289728 | tf_op jit(solution)/reshape | solution.py:58
Sparse Core Ops, SparseCore 0:
  203.1 50.2 reduce-scatter.28
  255.6 47.4 reduce-scatter.26
  306.0 47.4 reduce-scatter.24
  355.7 47.4 reduce-scatter.22
  406.0 47.4 reduce-scatter.20
  456.2 47.4 reduce-scatter.18
  529.0 44.5 all-gather.13
  575.7 45.0 all-gather.11
  623.0 45.0 all-gather.9
where the time goes:
time: 707 us; the launch traced here: 697 us
  waiting for transfers between devices  305 us (43%)
  matrix products  250 us (35%)
  other arithmetic  69.1 us (10%)
  local copies, waits for them, and re-layouts  40.5 us (6%)
  between operations  17.8 us (3%)
  blocking collectives  14 us (2%)
    unnamed x15, waiting for transfers between devices  178 us
    reshape x3, waiting for transfers between devices, step(): t.reshape(-1, *t.shape[2:])  127 us
    dot_general x5, matrix products, layer(): up = jnp.dot(a, w['w_up'], preferred_element_type=jnp.float32)  91.6 us
    dot_general x5, matrix products, layer(): gate = jnp.dot(a, w['w_gate'], preferred_element_type=jnp.float32)  82 us
    dot_general x5, matrix products, matmul(): jnp.dot(a, w, preferred_element_type=jnp.float32).astype(jnp.bfloat16)  76.3 us
    unnamed x31, local copies, waits for them, and re-layouts  40 us
    unnamed x4, other arithmetic  37.2 us
    reshape x3, other arithmetic, step(): t.reshape(-1, *t.shape[2:])  17.9 us
  transfers between devices with their start and end apart: 9, of which 7 were waited for; matrix products, arithmetic and copies ran while one was open for 19% of the time, Pallas kernels for 0%

commit v1 on v0

v1 whole, which is shorter than its diff:
```python
import functools

import jax
import jax.numpy as jnp
from jax import lax
from jax.experimental import pallas as pl
from jax.experimental.pallas import tpu as pltpu
from jax.sharding import PartitionSpec as P

F32, BF16 = jnp.float32, jnp.bfloat16
NT = (((1,), (1,)), ((), ()))

def dot(a, b):
    return jnp.dot(a, b, preferred_element_type=F32)
def dot_t(a, b):
    return lax.dot_general(a, b, NT, preferred_element_type=F32)

def norm_of(h):
    wide = h.astype(F32)
    scale = lax.rsqrt(jnp.mean(wide * wide, -1, keepdims=True) + 1e-6)
    return wide, scale

def tokens_kernel(nf, x_ref, dy_ref, wg_hbm, wu_hbm, wd_hbm, s_ref, a_ref, dh_ref, wg, wu, wd, g0, u0, sems):
    i = pl.program_id(0)
    ff = wg.shape[2]
    fb = ff // nf
    cols = [slice(k * fb, (k + 1) * fb) for k in range(nf)]
    hbm, vm = (wg_hbm, wu_hbm, wd_hbm), (wg, wu, wd)
    def copies(l):
        return [pltpu.make_async_copy(h.at[l], v.at[l], sems.at[l, j]) for j, (h, v) in enumerate(zip(hbm, vm))]
    @pl.when(i == 0)
    def _():
        for l in range(2):
            for c in copies(l): c.start()
    def arrive(l, j):
        @pl.when(i == 0)
        def _(): copies(l)[j].wait()

    x = x_ref[0]
    wide, scale = norm_of(x)
    a0 = (wide * scale).astype(BF16)
    a_ref[1] = a0
    arrive(0, 0); arrive(0, 1); arrive(0, 2)
    down = None
    for c in cols:
        g = dot(a0, wg[0, :, c]); u = dot(a0, wu[0, :, c])
        g0[:, c] = g; u0[:, c] = u
        p = (g * jax.nn.sigmoid(g) * u).astype(BF16)
        s_ref[5, :, c] = p
        d = dot(p, wd[0, c, :])
        down = d if down is None else down + d
    h1 = x + down.astype(BF16)
    wide1, scale1 = norm_of(h1)
    a1 = (wide1 * scale1).astype(BF16)
    a_ref[0] = a1
    dy = dy_ref[0]
    dh_ref[0] = dy
    arrive(1, 0); arrive(1, 1); arrive(1, 2)
    dag = dau = None
    for c in cols:
        g = dot(a1, wg[1, :, c]); u = dot(a1, wu[1, :, c])
        dp = dot_t(dy, wd[1, c, :]).astype(BF16).astype(F32)
        sig = jax.nn.sigmoid(g); si = g * sig
        s_ref[2, :, c] = (si * u).astype(BF16)
        dg = (dp * u * (sig + si * (1 - sig))).astype(BF16)
        du = (dp * si).astype(BF16)
        s_ref[0, :, c] = dg
        s_ref[1, :, c] = du
        e = dot_t(dg, wg[1, :, c]); f = dot_t(du, wu[1, :, c])
        dag = e if dag is None else dag + e
        dau = f if dau is None else dau + f
    da = (dag.astype(BF16) + dau.astype(BF16)).astype(F32)
    coef = jnp.sum(da * wide1, -1, keepdims=True) * (scale1 * scale1 * scale1) * (-1.0 / da.shape[-1])
    dh1 = dy + (da * scale1 + wide1 * coef).astype(BF16)
    dh_ref[1] = dh1
    for c in cols:
        dp = dot_t(dh1, wd[0, c, :]).astype(BF16).astype(F32)
        g = g0[:, c]; u = u0[:, c]
        sig = jax.nn.sigmoid(g); si = g * sig
        s_ref[3, :, c] = (dp * u * (sig + si * (1 - sig))).astype(BF16)
        s_ref[4, :, c] = (dp * si).astype(BF16)

def tokens(x, dy, wg, wu, wd, tm=256, nf=3):
    _, t, d = x.shape
    ff = wg.shape[2]
    tile = pl.BlockSpec((1, tm, d), lambda i: (0, i, 0))
    anyspec = pl.BlockSpec(memory_space=pl.ANY)
    return pl.pallas_call(
        functools.partial(tokens_kernel, nf), grid=(t // tm,),
        in_specs=[tile, tile, anyspec, anyspec, anyspec],
        out_specs=[pl.BlockSpec((6, tm, ff), lambda i: (0, i, 0)), pl.BlockSpec((2, tm, d), lambda i: (0, i, 0)), pl.BlockSpec((2, tm, d), lambda i: (0, i, 0))],
        out_shape=[jax.ShapeDtypeStruct((6, t, ff), BF16), jax.ShapeDtypeStruct((2, t, d), BF16), jax.ShapeDtypeStruct((2, t, d), BF16)],
        scratch_shapes=[pltpu.VMEM(wg.shape, BF16), pltpu.VMEM(wu.shape, BF16), pltpu.VMEM(wd.shape, BF16),
                        pltpu.VMEM((tm, ff), F32), pltpu.VMEM((tm, ff), F32), pltpu.SemaphoreType.DMA((2, 3))],
        compiler_params=pltpu.CompilerParams(vmem_limit_bytes=67043328, dimension_semantics=("arbitrary",)),
        name="tokens",
    )(x, dy, wg, wu, wd)


def adamw(w, m, v, g):
    m = 0.9 * m + 0.1 * g
    v = 0.95 * v + 0.05 * g * g
    step = m * lax.rsqrt(v + 1e-8) + 0.1 * w
    return (w - 0.02 * step).astype(BF16), m, v


def solution(mesh):
    n = mesh.shape["dp"]

    def step(x, dy, wg, wu, wd, mg, mu, md, vg, vu, vd):
        s, a, dh = tokens(x, dy, wg, wu, wd)

        def grad(lhs, rhs):
            term = lax.dot_general(lhs, rhs, (((0,), (0,)), ((), ())), preferred_element_type=F32).astype(BF16)
            return lax.psum_scatter(term, "dp", scatter_dimension=0, tiled=True).astype(F32)

        first, last = {}, {}
        for to, l in ((last, 0), (first, 1)):
            to["g"] = grad(a[l], s[3 * l])
            to["u"] = grad(a[l], s[3 * l + 1])
            to["d"] = grad(s[3 * l + 2], dh[l])
        grads = [jnp.stack([first[k], last[k]]) for k in "gud"]
        count = n * sum(g.size for g in grads)
        total = lax.psum(sum(jnp.sum(g * g) for g in grads), "dp")
        factor = jnp.minimum(1.0, 0.5 * lax.rsqrt(total / count + 1e-30))
        me = lax.axis_index("dp")
        new = []
        for w, m, v, g in zip((wg, wu, wd), (mg, mu, md), (vg, vu, vd), grads):
            rows = m.shape[1]
            own = lax.dynamic_slice_in_dim(w, me * rows, rows, 1).astype(F32)
            nw, nm, nv = adamw(own, m, v, g * factor)
            new.append((lax.all_gather(nw, "dp", axis=1, tiled=True), nm, nv))
        return tuple(one[i] for i in range(3) for one in new)

    data, whole, rows = P(("rep", "dp"), None, None), P(None, None, None), P(None, "dp", None)
    return jax.shard_map(step, mesh=mesh, in_specs=(data,) * 2 + (whole,) * 3 + (rows,) * 6,
                         out_specs=(P("rep", None, None),) * 3 + (P("rep", "dp", None),) * 6, check_vma=False)
```

time: 707 us -> 546 us (0.77)
  matrix products: 250 us -> 90.4 us
  Pallas kernels: 0 us -> 113 us
  waiting for transfers between devices: 305 us -> 256 us
  other arithmetic: 69.1 us -> 23.7 us
  local copies, waits for them, and re-layouts: 40.5 us -> 21.8 us
    unnamed x15 -> x9, waiting for transfers between devices: 178 us -> 0.48 us
    dot_general x15 -> x6, matrix products: 250 us -> 90.4 us  [grad(): lax.dot_general(lhs, rhs, (((0,), (0,)), ((), ())), preferred_element_typ...]
    all_gather x0 -> x3, waiting for transfers between devices: none -> 128 us  [step(): new.append((lax.all_gather(nw, 'dp', axis=1, tiled=True), nm, nv))]
    reduce_scatter x0 -> x6, waiting for transfers between devices: none -> 128 us  [grad(): lax.psum_scatter(term, 'dp', scatter_dimension=0, tiled=True).astype(F32)]
    reshape x3 -> x0, waiting for transfers between devices: 127 us -> none  [step(): t.reshape(-1, *t.shape[2:])]
    pallas_call x0 -> x1, Pallas kernels: none -> 113 us  [tokens(): pl.pallas_call(functools.partial(tokens_kernel, nf), grid=(t // tm,), in_...]
    unnamed x4 -> x0, other arithmetic: 37.2 us -> none
    unnamed x31 -> x11, local copies, waits for them, and re-layouts: 40 us -> 21.8 us
  transfers between devices with their start and end apart: 9 -> 9, of which waited for: 7 -> 7; matrix products, arithmetic and copies ran while one was open for 19% -> 17% of each run, Pallas kernels for 0% -> 0%
where the time goes in v1:
time: 546 us; the launch traced here: 539 us
  waiting for transfers between devices  256 us (47%)
  Pallas kernels  113 us (21%)
  matrix products  90.4 us (17%)
  other arithmetic  23.7 us (4%)
  local copies, waits for them, and re-layouts  21.8 us (4%)
  between operations  17.1 us (3%)
  blocking collectives  15.9 us (3%)
    all_gather x3, waiting for transfers between devices, step(): new.append((lax.all_gather(nw, 'dp', axis=1, tiled=True), nm, nv))  128 us
    reduce_scatter x6, waiting for transfers between devices, grad(): lax.psum_scatter(term, 'dp', scatter_dimension=0, tiled=True).astype(F32)  128 us
    pallas_call x1, Pallas kernels, tokens(): pl.pallas_call(functools.partial(tokens_kernel, nf), grid=(t // tm,), in_...  113 us
    dot_general x6, matrix products, grad(): lax.dot_general(lhs, rhs, (((0,), (0,)), ((), ())), preferred_element_typ...  90.4 us
    unnamed x11, local copies, waits for them, and re-layouts  21.8 us
    convert_element_type x3, other arithmetic, adamw(): return ((w - 0.02 * step).astype(BF16), m, v)  16.7 us
    psum x1, blocking collectives, step(): total = lax.psum(sum((jnp.sum(g * g) for g in grads)), 'dp')  15.9 us
  transfers between devices with their start and end apart: 9, of which 7 were waited for; matrix products, arithmetic and copies ran while one was open for 17% of the time, Pallas kernels for 0%

profile of v1, /device:TPU:113, one launch (start us, length us, event | category | flops | bytes accessed | tf_op | source)
XLA Modules:
  0.0 538.6 jit_solution(17330102648085471965)
XLA Ops:
  7.3 112.9 %tokens.1 = (bf16[6,2048,2304]{2,1,0:T(8,128)(2,1)}, bf16[2,2048,896]{2,1,0:T(8,128)(2,1)}, bf16[2,2048,896]{2,1,0:T(8,128)(2,1)}) custom-call(bf16[1,2048,896]{2,1,0:T(8,128)(2,1)} %x_ref.1, bf16[1,2048,896]{2,1,0:T(8,128)(2,1)} %dy_ref.1, bf16[2,896,2304]{2,1,0:T(8,128)(2,1)} %wg_hbm.1, bf16[2,896,2304]{2,1,0:T(8,128)(2,1)} %wu_hbm.1, ...), custom_call_target="tpu_custom_call" | custom-call | tf_op jit(solution)/shard_map/tokens/pallas_call | solution.py:88
  120.1 15.3 %fusion.24 = bf16[896,2304]{1,0:T(8,128)(2,1)} fusion(bf16[6,2048,2304]{2,1,0:T(8,128)(2,1)} %get-tuple-element.13, bf16[2,2048,896]{2,1,0:T(8,128)(2,1)} %get-tuple-element.12), kind=kOutput, calls=%fused_computation.20 | convolution fusion | flops 8457781248 | bytes 17235968 | tf_op jit(solution)/shard_map/dot_general | solution.py:114
  135.5 0.1 reduce-scatter.13.cloned.1.call-start
  135.6 14.9 %fusion.27 = bf16[896,2304]{1,0:T(8,128)(2,1)} fusion(bf16[6,2048,2304]{2,1,0:T(8,128)(2,1)} %get-tuple-element.13, bf16[2,2048,896]{2,1,0:T(8,128)(2,1)} %get-tuple-element.12), kind=kOutput, calls=%fused_computation.21 | convolution fusion | flops 8457781248 | bytes 17235968 | tf_op jit(solution)/shard_map/dot_general | solution.py:114
  150.6 0.1 reduce-scatter.7.cloned.1.call-start
  150.6 15.1 %fusion.18 = bf16[896,2304]{1,0:T(8,128)(2,1)} fusion(bf16[6,2048,2304]{2,1,0:T(8,128)(2,1)} %get-tuple-element.13, bf16[2,2048,896]{2,1,0:T(8,128)(2,1)} %get-tuple-element.12), kind=kOutput, calls=%fused_computation.18 | convolution fusion | flops 8457781248 | bytes 17235968 | tf_op jit(solution)/shard_map/dot_general | solution.py:114
  165.8 0.1 reduce-scatter.9.cloned.1.call-start
  165.8 14.8 %fusion.21 = bf16[896,2304]{1,0:T(8,128)(2,1)} fusion(bf16[6,2048,2304]{2,1,0:T(8,128)(2,1)} %get-tuple-element.13, bf16[2,2048,896]{2,1,0:T(8,128)(2,1)} %get-tuple-element.12), kind=kOutput, calls=%fused_computation.19 | convolution fusion | flops 8457781248 | bytes 17235968 | tf_op jit(solution)/shard_map/dot_general | solution.py:114
  180.7 0.1 reduce-scatter.15.cloned.1.call-start
  180.8 15.3 %fusion.30 = bf16[2304,896]{1,0:T(8,128)(2,1)} fusion(bf16[6,2048,2304]{2,1,0:T(8,128)(2,1)} %get-tuple-element.13, bf16[2,2048,896]{2,1,0:T(8,128)(2,1)} %get-tuple-element.14), kind=kOutput, calls=%fused_computation.22 | convolution fusion | flops 8457781248 | bytes 17235968 | tf_op jit(solution)/shard_map/dot_general | solution.py:114
  196.1 0.1 reduce-scatter.17.cloned.1.call-start
  196.2 15.0 %fusion.33 = bf16[2304,896]{1,0:T(8,128)(2,1)} fusion(bf16[6,2048,2304]{2,1,0:T(8,128)(2,1)} %get-tuple-element.13, bf16[2,2048,896]{2,1,0:T(8,128)(2,1)} %get-tuple-element.14), kind=kOutput, calls=%fused_computation.23 | convolution fusion | flops 8457781248 | bytes 17235968 | tf_op jit(solution)/shard_map/dot_general | solution.py:114
  211.2 0.1 all-gather.8.cloned.1.call-start
  211.4 2.3 fusion.58
  213.7 25.7 %reduce-scatter.7.cloned.1.call-done = bf16[112,2304]{1,0:T(8,128)(2,1)} async-done(((bf16[896,2304]{1,0:T(8,128)(2,1)}), bf16[112,2304]{1,0:T(8,128)(2,1)}) %reduce-scatter.7.cloned.1.call-update) | async-done | bytes 516112 | tf_op jit(solution)/shard_map/reduce_scatter | solution.py:115
  239.4 35.4 %reduce-scatter.9.cloned.1.call-done = bf16[112,2304]{1,0:T(8,128)(2,1)} async-done(((bf16[896,2304]{1,0:T(8,128)(2,1)}), bf16[112,2304]{1,0:T(8,128)(2,1)}) %reduce-scatter.9.cloned.1.call-update) | async-done | bytes 516112 | tf_op jit(solution)/shard_map/reduce_scatter | solution.py:115
  274.8 2.3 fusion.57
  278.5 31.2 %reduce-scatter.15.cloned.1.call-done = bf16[288,896]{1,0:T(8,128)(2,1)} async-done(((bf16[2304,896]{1,0:T(8,128)(2,1)}), bf16[288,896]{1,0:T(8,128)(2,1)}) %reduce-scatter.15.cloned.1.call-update) | async-done | bytes 516112 | tf_op jit(solution)/shard_map/reduce_scatter | solution.py:115
  309.6 35.4 %reduce-scatter.17.cloned.1.call-done = bf16[288,896]{1,0:T(8,128)(2,1)} async-done(((bf16[2304,896]{1,0:T(8,128)(2,1)}), bf16[288,896]{1,0:T(8,128)(2,1)}) %reduce-scatter.17.cloned.1.call-update) | async-done | bytes 516112 | tf_op jit(solution)/shard_map/reduce_scatter | solution.py:115
  345.0 2.3 fusion.59
  348.0 15.9 %psum.7 = f32[]{:T(128)} all-reduce(f32[]{:T(128)S(6)} %add.71), channel_id=1, replica_groups=mesh['rep'=2,'dp'=8] {'dp'}, use_global_device_ids=true, to_apply=%region_9.0 | all-reduce | flops 1 | bytes 8 | tf_op jit(solution)/shard_map/psum | solution.py:124
  364.6 5.8 %fusion.65 = (bf16[2,288,896]{2,1,0:T(8,128)(2,1)}, f32[2,288,896]{2,1,0:T(8,128)}, f32[2,288,896]{2,1,0:T(8,128)}) fusion(bf16[2,2304,896]{2,1,0:T(8,128)(2,1)} %wd_hbm.1, s32[]{:T(128)S(6)} %select_n.8, f32[]{:T(128)S(6)} %min_shard_map.3, bf16[1,288,896]{2,1,0:T(8,128)(2,1)} %bitcast.63, bf16[1,288,896]{2,1,0:T(8,128)(2,1)} %bitcast.61, ...), kind=kLoop, calls=%fused_computation.68 | loop fusion | flops 10321920 | bytes 11354120 | tf_op jit(solution)/shard_map/convert_element_type | solution.py:104
  370.5 0.3 all-gather.6.cloned.1.call-start
  370.9 5.5 %fusion.62 = (bf16[2,112,2304]{2,1,0:T(8,128)(2,1)}, f32[2,112,2304]{2,1,0:T(8,128)}, f32[2,112,2304]{2,1,0:T(8,128)}) fusion(bf16[2,896,2304]{2,1,0:T(8,128)(2,1)} %wu_hbm.1, s32[]{:T(128)S(6)} %select_n.7, f32[]{:T(128)S(6)} %min_shard_map.3, bf16[1,112,2304]{2,1,0:T(8,128)(2,1)S(1)} %bitcast.57, bf16[1,112,2304]{2,1,0:T(8,128)(2,1)S(1)} %bitcast.53, ...), kind=kLoop, calls=%fused_computation.65 | loop fusion | flops 10321920 | bytes 11354120 | tf_op jit(solution)/shard_map/convert_element_type | solution.py:104
  376.4 0.1 all-gather.4.cloned.1.call-start
  376.5 5.4 %fusion.56 = (bf16[2,112,2304]{2,1,0:T(8,128)(2,1)}, f32[2,112,2304]{2,1,0:T(8,128)}, f32[2,112,2304]{2,1,0:T(8,128)}) fusion(bf16[2,896,2304]{2,1,0:T(8,128)(2,1)} %wg_hbm.1, s32[]{:T(128)S(6)} %select_n.7, f32[]{:T(128)S(6)} %min_shard_map.3, bf16[1,112,2304]{2,1,0:T(8,128)(2,1)S(1)} %bitcast.59, bf16[1,112,2304]{2,1,0:T(8,128)(2,1)S(1)} %bitcast.55, ...), kind=kLoop, calls=%fused_computation.59 | loop fusion | flops 10321920 | bytes 11354120 | tf_op jit(solution)/shard_map/convert_element_type | solution.py:104
  382.0 33.3 %all-gather.8.cloned.1.call-done = bf16[2,2304,896]{2,1,0:T(8,128)(2,1)} async-done(((bf16[2,288,896]{2,1,0:T(8,128)(2,1)}), bf16[2,2304,896]{2,1,0:T(8,128)(2,1)}) %all-gather.8.cloned.1.call-update) | async-done | bytes 8257552 | tf_op jit(solution)/shard_map/all_gather | solution.py:132
  415.2 47.3 %all-gather.6.cloned.1.call-done = bf16[2,896,2304]{2,1,0:T(8,128)(2,1)} async-done(((bf16[2,112,2304]{2,1,0:T(8,128)(2,1)}), bf16[2,896,2304]{2,1,0:T(8,128)(2,1)}) %all-gather.6.cloned.1.call-update) | async-done | bytes 8257552 | tf_op jit(solution)/shard_map/all_gather | solution.py:132
  462.5 47.3 %all-gather.4.cloned.1.call-done = bf16[2,896,2304]{2,1,0:T(8,128)(2,1)} async-done(((bf16[2,112,2304]{2,1,0:T(8,128)(2,1)}), bf16[2,896,2304]{2,1,0:T(8,128)(2,1)}) %all-gather.4.cloned.1.call-update) | async-done | bytes 8257552 | tf_op jit(solution)/shard_map/all_gather | solution.py:132
  509.8 7.2 %copy.23 = bf16[2,896,2304]{2,1,0:T(8,128)(2,1)} copy(bf16[2,896,2304]{2,1,0:T(8,128)(2,1)} %all-gather.4.cloned.1.call-done) | data formatting | bytes 16515072
  517.0 7.2 %copy.24 = bf16[2,896,2304]{2,1,0:T(8,128)(2,1)} copy(bf16[2,896,2304]{2,1,0:T(8,128)(2,1)} %all-gather.6.cloned.1.call-done) | data formatting | bytes 16515072
  524.3 7.3 %copy.25 = bf16[2,2304,896]{2,1,0:T(8,128)(2,1)} copy(bf16[2,2304,896]{2,1,0:T(8,128)(2,1)} %all-gather.8.cloned.1.call-done) | data formatting | bytes 16515072
  (20 shorter events, 0.6 us)
Async XLA Ops:
  7.2 204.1 %reduce-scatter.11.cloned.1.call-start = ((), (), s32[]{:S(2)}) async-start(), calls=%async_computation.8 | async-start | bytes 4644864 | tf_op jit(solution)/shard_map/reduce_scatter | solution.py:115
  135.5 75.8 %reduce-scatter.13.cloned.1.call-start = ((), (), s32[]{:S(2)}) async-start(), calls=%async_computation.9 | async-start | bytes 4644864 | tf_op jit(solution)/shard_map/reduce_scatter | solution.py:115
  150.6 88.9 %reduce-scatter.7.cloned.1.call-start = ((), (), s32[]{:S(2)}) async-start(), calls=%async_computation.6 | async-start | bytes 4644864 | tf_op jit(solution)/shard_map/reduce_scatter | solution.py:115
  165.8 109.1 %reduce-scatter.9.cloned.1.call-start = ((), (), s32[]{:S(2)}) async-start(), calls=%async_computation.7 | async-start | bytes 4644864 | tf_op jit(solution)/shard_map/reduce_scatter | solution.py:115
  180.7 128.9 %reduce-scatter.15.cloned.1.call-start = ((), (), s32[]{:S(2)}) async-start(), calls=%async_computation.10 | async-start | bytes 4644864 | tf_op jit(solution)/shard_map/reduce_scatter | solution.py:115
  196.1 148.9 %reduce-scatter.17.cloned.1.call-start = ((), (), s32[]{:S(2)}) async-start(), calls=%async_computation.11 | async-start | bytes 4644864 | tf_op jit(solution)/shard_map/reduce_scatter | solution.py:115
  211.2 204.0 %all-gather.8.cloned.1.call-start = ((), (), s32[]{:S(2)}) async-start(), calls=%async_computation.14 | async-start | bytes 9289728 | tf_op jit(solution)/shard_map/all_gather | solution.py:132
  364.6 6.2 %copy-start = (bf16[112,2304]{1,0:T(8,128)(2,1)S(1)}, bf16[112,2304]{1,0:T(8,128)(2,1)}, u32[]{:S(2)}) copy-start(bf16[112,2304]{1,0:T(8,128)(2,1)} %reduce-scatter.11.cloned.1.call-done) | copy-start | bytes 1548292
  364.6 6.2 %copy-start.2 = (bf16[112,2304]{1,0:T(8,128)(2,1)S(1)}, bf16[112,2304]{1,0:T(8,128)(2,1)}, u32[]{:S(2)}) copy-start(bf16[112,2304]{1,0:T(8,128)(2,1)} %reduce-scatter.13.cloned.1.call-done) | copy-start | bytes 1548292
  370.5 92.0 %all-gather.6.cloned.1.call-start = ((), (), s32[]{:S(2)}) async-start(), calls=%async_computation.13 | async-start | bytes 9289728 | tf_op jit(solution)/shard_map/all_gather | solution.py:132
  370.9 5.6 %copy-start.1 = (bf16[112,2304]{1,0:T(8,128)(2,1)S(1)}, bf16[112,2304]{1,0:T(8,128)(2,1)}, u32[]{:S(2)}) copy-start(bf16[112,2304]{1,0:T(8,128)(2,1)} %reduce-scatter.7.cloned.1.call-done) | copy-start | bytes 1548292
  370.9 5.6 %copy-start.3 = (bf16[112,2304]{1,0:T(8,128)(2,1)S(1)}, bf16[112,2304]{1,0:T(8,128)(2,1)}, u32[]{:S(2)}) copy-start(bf16[112,2304]{1,0:T(8,128)(2,1)} %reduce-scatter.9.cloned.1.call-done) | copy-start | bytes 1548292
  376.4 133.4 %all-gather.4.cloned.1.call-start = ((), (), s32[]{:S(2)}) async-start(), calls=%async_computation.12 | async-start | bytes 9289728 | tf_op jit(solution)/shard_map/all_gather | solution.py:132
Sparse Core Ops, SparseCore 0:
  135.7 33.7 reduce-scatter.10
  171.8 32.6 reduce-scatter.12
  206.8 32.5 reduce-scatter.6
  242.2 32.5 reduce-scatter.8
  277.0 32.5 reduce-scatter.14
  312.4 32.5 reduce-scatter.16
  370.6 44.5 all-gather.7
  417.4 45.0 all-gather.5
  464.7 45.0 all-gather.3

commit v2 on v1

--- a/solution.py
+++ b/solution.py
@@ -39,7 +39,7 @@
     x = x_ref[0]
     wide, scale = norm_of(x)
     a0 = (wide * scale).astype(BF16)
-    a_ref[1] = a0
+    a_ref[1] = a0.T
     arrive(0, 0); arrive(0, 1); arrive(0, 2)
     down = None
     for c in cols:
@@ -52,7 +52,7 @@
     h1 = x + down.astype(BF16)
     wide1, scale1 = norm_of(h1)
     a1 = (wide1 * scale1).astype(BF16)
-    a_ref[0] = a1
+    a_ref[0] = a1.T
     dy = dy_ref[0]
     dh_ref[0] = dy
     arrive(1, 0); arrive(1, 1); arrive(1, 2)
@@ -88,49 +88,340 @@
     return pl.pallas_call(
         functools.partial(tokens_kernel, nf), grid=(t // tm,),
         in_specs=[tile, tile, anyspec, anyspec, anyspec],
-        out_specs=[pl.BlockSpec((6, tm, ff), lambda i: (0, i, 0)), pl.BlockSpec((2, tm, d), lambda i: (0, i, 0)), pl.BlockSpec((2, tm, d), lambda i: (0, i, 0))],
-        out_shape=[jax.ShapeDtypeStruct((6, t, ff), BF16), jax.ShapeDtypeStruct((2, t, d), BF16), jax.ShapeDtypeStruct((2, t, d), BF16)],
+        out_specs=[pl.BlockSpec((6, tm, ff), lambda i: (0, i, 0)), pl.BlockSpec((2, d, tm), lambda i: (0, 0, i)), pl.BlockSpec((2, tm, d), lambda i: (0, i, 0))],
+        out_shape=[jax.ShapeDtypeStruct((6, t, ff), BF16), jax.ShapeDtypeStruct((2, d, t), BF16), jax.ShapeDtypeStruct((2, t, d), BF16)],
         scratch_shapes=[pltpu.VMEM(wg.shape, BF16), pltpu.VMEM(wu.shape, BF16), pltpu.VMEM(wd.shape, BF16),
                         pltpu.VMEM((tm, ff), F32), pltpu.VMEM((tm, ff), F32), pltpu.SemaphoreType.DMA((2, 3))],
         compiler_params=pltpu.CompilerParams(vmem_limit_bytes=67043328, dimension_semantics=("arbitrary",)),
         name="tokens",
     )(x, dy, wg, wu, wd)
-
-
-def adamw(w, m, v, g):
-    m = 0.9 * m + 0.1 * g
-    v = 0.95 * v + 0.05 * g * g
-    step = m * lax.rsqrt(v + 1e-8) + 0.1 * w
-    return (w - 0.02 * step).astype(BF16), m, v
-
+TN = (((0,), (0,)), ((), ()))
+NK = 3
+RING = 11
+
+def grads_kernel(n, s_hbm, at_hbm, dh_hbm, g_ref, ss_ref, at, dh, inb, st, re, sb, rt, cb, rf, ss, ssr,
+                 in_sem, ld_sem, e_s, e_r, r1_s, r1_r, r2_s, r2_r, x_s, x_r):
+    me = lax.axis_index("dp")
+    core, chip = lax.rem(me, 2), lax.div(me, 2)
+    chips = n // 2
+    mats, t, ff = s_hbm.shape
+    d = at_hbm.shape[1]
+    chunks = mats * NK
+    cw, rg, rk = ff // NK, d // n, ff // n // NK
+    rows = g_ref.shape[1]
+    half = rows // 2
+    A, B = pl.ds(0, half), pl.ds(half, half)
+    nxt, prv, far = lax.rem(chip + 1, chips), lax.rem(chip + chips - 1, chips), lax.rem(chip + 2, chips)
+    right, left, partner = nxt * 2 + core, prv * 2 + core, chip * 2 + (1 - core)
+
+    def remote(src, dst, send, recv, to):
+        return pltpu.make_async_remote_copy(src_ref=src, dst_ref=dst, send_sem=send, recv_sem=recv,
+                                            device_id={"dp": to}, device_id_type=pl.DeviceIdType.MESH)
+
+    def fetch(c):
+        return pltpu.make_async_copy(s_hbm.at[lax.div(c, NK), :, pl.ds(pl.multiple_of(lax.rem(c, NK) * cw, cw), cw)],
+                                     inb.at[lax.rem(c, 2)], in_sem.at[lax.rem(c, 2)])
+
+    def loads(l):
+        return (pltpu.make_async_copy(at_hbm.at[l], at, ld_sem.at[0]), pltpu.make_async_copy(dh_hbm.at[l], dh, ld_sem.at[1]))
+
+    fetch(0).start()
+    barrier = pltpu.get_barrier_semaphore()
+    for o in range(1, n):
+        pl.semaphore_signal(barrier, inc=1, device_id={"dp": lax.rem(me + o, n)}, device_id_type=pl.DeviceIdType.MESH)
+    pl.semaphore_wait(barrier, n - 1)
+    ss[...] = jnp.zeros_like(ss)
+
+    def compute(c, _):
+        mat, k = lax.div(c, NK), lax.rem(c, NK)
+        layer, kind = lax.div(mat, 3), lax.rem(mat, 3)
+        fresh = lax.rem(c, 3 * NK) == 0
+
+        @pl.when(fresh)
+        def _():
+            for one in loads(layer):
+                one.start()
+        fetch(c).wait()
+
+        @pl.when(c + 1 < chunks)
+        def _():
+            fetch(c + 1).start()
+
+        @pl.when(fresh)
+        def _():
+            for one in loads(layer):
+                one.wait()
+        slot = lax.rem(c, 2)
+
+        @pl.when(kind < 2)
+        def _():
+            def sub(j, _):
+                out = jnp.dot(at[...], inb[slot, :, pl.ds(pl.multiple_of(j * 256, 256), 256)], preferred_element_type=F32).astype(BF16)
+                for b in range(n):
+                    for i in range(2):
+                        st[lax.rem(core + b, 2), lax.rem(c, RING), b // 2, pl.ds(pl.multiple_of((2 * j + i) * rg, 16), rg), :] = \
+                            out[b * rg:(b + 1) * rg, i * 128:(i + 1) * 128]
+                return 0
+            lax.fori_loop(0, cw // 256, sub, 0)
+
+        @pl.when(kind == 2)
+        def _():
+            def sub(j, _):
+                wide = cw // 2
+                out = lax.dot_general(inb[slot, :, pl.ds(pl.multiple_of(j * wide, 128), wide)], dh[...], TN, preferred_element_type=F32).astype(BF16)
+                for i in range(wide // rk):
+                    q = (2 * k + j) * (wide // rk) + i
+                    b, part = lax.div(q, NK), lax.rem(q, NK)
+                    for tile in range(d // 128):
+                        st[lax.rem(core + b, 2), lax.rem(mat * NK + part, RING), lax.div(b, 2), tile * rk:(tile + 1) * rk, :] = \
+                            out[i * rk:(i + 1) * rk, tile * 128:(tile + 1) * 128]
+                return 0
+            lax.fori_loop(0, 2, sub, 0)
+        return 0
+
+    def exchange(c):
+        return remote(st.at[1, lax.rem(c, RING)], re.at[c], e_s.at[lax.rem(c, 4)], e_r.at[c], partner)
+
+    def first(c):
+        r, q = lax.rem(c, 3), lax.rem(c, 4)
+        return (remote(sb.at[r, 0], rt.at[c, 0], r1_s.at[q, 0], r1_r.at[c, 0], left),
+                remote(sb.at[r, 1], rt.at[c, 1], r1_s.at[q, 1], r1_r.at[c, 1], right),
+                remote(sb.at[r, 2], rf.at[c, 0, B], r1_s.at[q, 2], r1_r.at[c, 2], left),
+                remote(sb.at[r, 3], rf.at[c, 1, A], r1_s.at[q, 3], r1_r.at[c, 3], right))
+
+    def second(c):
+        r, q = lax.rem(c, 3), lax.rem(c, 4)
+        return (remote(cb.at[r, 0], rf.at[c, 0, A], r2_s.at[q, 0], r2_r.at[c, 0], left),
+                remote(cb.at[r, 1], rf.at[c, 1, B], r2_s.at[q, 1], r2_r.at[c, 1], right))
+
+    def pair(c, to, part):
+        return st[0, lax.rem(c, RING), to, part, :].astype(F32) + re[c, to, part, :].astype(F32)
+
+    def step(s, _):
+        def done(u):
+            ahead = jnp.where(u >= 5, 1, 0) + jnp.where(u >= 6, 1, 0)
+            return jnp.minimum(u + 1 + ahead, chunks)
+        lax.fori_loop(jnp.where(s == 0, 0, done(s - 1)), done(s), compute, 0)
+
+        @pl.when((s >= 2) & (s < chunks + 2))
+        def _():
+            c = s - 2
+            exchange(c).wait()
+            r = lax.rem(c, 3)
+            sb[r, 0] = pair(c, far, A).astype(BF16)
+            sb[r, 1] = pair(c, far, B).astype(BF16)
+            sb[r, 2] = pair(c, prv, B).astype(BF16)
+            sb[r, 3] = pair(c, nxt, A).astype(BF16)
+
+        @pl.when((s >= 4) & (s < chunks + 4))
+        def _():
+            c = s - 4
+            for i, one in enumerate(first(c)):
+                one.wait_send()
+                if i < 2:
+                    one.wait_recv()
+            r = lax.rem(c, 3)
+            cb[r, 0] = (pair(c, prv, A) + rt[c, 0].astype(F32)).astype(BF16)
+            cb[r, 1] = (pair(c, nxt, B) + rt[c, 1].astype(F32)).astype(BF16)
+
+        @pl.when(s < chunks)
+        def _():
+            exchange(s).start()
+
+        @pl.when((s >= 4) & (s < chunks + 4))
+        def _():
+            for one in second(s - 4):
+                one.start()
+
+        @pl.when((s >= 2) & (s < chunks + 2))
+        def _():
+            for one in first(s - 2):
+                one.start()
+
+        @pl.when(s >= 6)
+        def _():
+            c = s - 6
+            for one in first(c)[2:]:
+                one.wait_recv()
+            for one in second(c):
+                one.wait()
+            g = (pair(c, chip, pl.ds(0, rows)) + rf[c, 0].astype(F32) + rf[c, 1].astype(F32)).astype(BF16)
+            g_ref[c] = g
+            wide = g.astype(F32)
+            ss[...] += jnp.sum((wide * wide).reshape(rows // 8, 8, 128), 0)
+        return 0
+
+    lax.fori_loop(0, chunks + 6, step, 0)
+    tell = [remote(ss, ssr.at[o], x_s.at[o], x_r.at[o], lax.rem(me + o, n)) for o in range(1, n)]
+    for one in tell:
+        one.start()
+    total = ss[...]
+    for o, one in enumerate(tell, 1):
+        one.wait()
+        total = total + ssr[o]
+    ss_ref[...] = total
+
+def grads(n, s, at, dh):
+    mats, t, ff = s.shape
+    d = at.shape[1]
+    chunks, rows = mats * NK, ff // NK // 128 * (d // n)
+    assert rows == d // 128 * (ff // n // NK)
+    half, dma = rows // 2, pltpu.SemaphoreType.DMA
+    anyspec = pl.BlockSpec(memory_space=pl.ANY)
+    return pl.pallas_call(
+        functools.partial(grads_kernel, n),
+        in_specs=[anyspec] * 3,
+        out_specs=[pl.BlockSpec(memory_space=pltpu.VMEM)] * 2,
+        out_shape=[jax.ShapeDtypeStruct((chunks, rows, 128), BF16), jax.ShapeDtypeStruct((8, 128), F32)],
+        scratch_shapes=[pltpu.VMEM((d, t), BF16), pltpu.VMEM((t, d), BF16), pltpu.VMEM((2, t, ff // NK), BF16),
+                        pltpu.VMEM((2, RING, n // 2, rows, 128), BF16), pltpu.VMEM((chunks, n // 2, rows, 128), BF16),
+                        pltpu.VMEM((3, 4, half, 128), BF16), pltpu.VMEM((chunks, 2, half, 128), BF16),
+                        pltpu.VMEM((3, 2, half, 128), BF16), pltpu.VMEM((chunks, 2, rows, 128), BF16),
+                        pltpu.VMEM((8, 128), F32), pltpu.VMEM((n, 8, 128), F32),
+                        dma((2,)), dma((2,)), dma((4,)), dma((chunks,)), dma((4, 4)), dma((chunks, 4)), dma((4, 2)), dma((chunks, 2)),
+                        dma((n,)), dma((n,))],
+        compiler_params=pltpu.CompilerParams(vmem_limit_bytes=67043328, collective_id=0, has_side_effects=True),
+        name="grads",
+    )(s, at, dh)
+
+def adam_kernel(count, me_ref, ss_ref, g_ref, *refs):
+    ws, ms, vs, outs = refs[:3], refs[3:6], refs[6:9], refs[9:]
+    total = jnp.sum(ss_ref[...], keepdims=True)
+    factor = jnp.minimum(1.0, 0.5 * lax.rsqrt(total / count + 1e-30))
+    for i in range(3):
+        rows, cols = ms[i].shape[1:]
+        for t in range(cols // 128):
+            c = slice(t * 128, (t + 1) * 128)
+            g = g_ref[0, i, 0, t * rows:(t + 1) * rows, :].astype(F32) * factor
+            m = 0.9 * ms[i][0, :, c] + 0.1 * g
+            v = 0.95 * vs[i][0, :, c] + 0.05 * g * g
+            w = ws[i][0, :, c].astype(F32)
+            outs[i][0, :, c] = (w - 0.02 * (m * lax.rsqrt(v + 1e-8) + 0.1 * w)).astype(BF16)
+            outs[3 + i][0, :, c] = m
+            outs[6 + i][0, :, c] = v
+
+def adam(n, me, ss, g, ws, ms, vs):
+    layers, d, ff = ws[0].shape
+    rg, rk, cw = d // n, ff // n // NK, ff // NK
+    wide = lambda at: pl.BlockSpec((1, rg, cw), lambda l, k, me: (l, at(me), k))
+    tall = lambda at: pl.BlockSpec((1, rk, d), lambda l, k, me: (l, NK * at(me) + k, 0))
+    none, mine = (lambda me: 0), (lambda me: me[0])
+    three = lambda at: [wide(at), wide(at), tall(at)]
+    shapes = lambda dt: [jax.ShapeDtypeStruct(m.shape, dt) for m in ms]
+    grid = pltpu.PrefetchScalarGridSpec(
+        num_scalar_prefetch=1, grid=(layers, NK),
+        in_specs=[pl.BlockSpec((8, 128), lambda l, k, me: (0, 0)),
+                  pl.BlockSpec((1, 3, 1) + g.shape[1:], lambda l, k, me: (layers - 1 - l, 0, k, 0, 0))]
+        + three(mine) + three(none) * 2,
+        out_specs=three(none) * 3)
+    count = n * sum(m.size for m in ms)
+    out = pl.pallas_call(functools.partial(adam_kernel, count), grid_spec=grid, out_shape=shapes(BF16) + shapes(F32) * 2,
+                         compiler_params=pltpu.CompilerParams(vmem_limit_bytes=40 << 20), name="adam",
+                         )(me, ss, g.reshape((layers, 3, NK) + g.shape[1:]), *ws, *ms, *vs)
+    return out[:3], out[3:6], out[6:]
+
+def gather_kernel(n, *refs):
+    mine, outs, (in_sem, s_sem, r_sem) = refs[:3], refs[3:6], refs[6:]
+    me = lax.axis_index("dp")
+    chips = n // 2
+    core, chip = lax.rem(me, 2), lax.div(me, 2)
+    owner = lambda c, q=None: lax.rem(c + chips, chips) * 2 + (core if q is None else q)
+    right, left, partner = owner(chip + 1), owner(chip - 1), owner(chip, 1 - core)
+    pieces = [(i, l) for l in range(2) for i in range(3)]
+
+    def place(i, l, b):
+        rows = mine[i].shape[1]
+        return outs[i].at[l, pl.ds(pl.multiple_of(b * rows, 16), rows), :]
+    own = [pltpu.make_async_copy(mine[i].at[l], place(i, l, me), in_sem.at[p]) for p, (i, l) in enumerate(pieces)]
+    for one in own:
+        one.start()
+    barrier = pltpu.get_barrier_semaphore()
+    for to in (left, right, partner):
+        pl.semaphore_signal(barrier, inc=1, device_id={"dp": to}, device_id_type=pl.DeviceIdType.MESH)
+    pl.semaphore_wait(barrier, 3)
+    for one in own:
+        one.wait()
+
+    def copy(kind, p, there=False):
+        i, l = pieces[p]
+        far_right = l == 0
+        if kind == 0:
+            to, b = right, me
+        elif kind == 1:
+            to, b = left, me
+        elif kind == 2:
+            to, b = (right, owner(chip - 1)) if far_right else (left, owner(chip + 1))
+        else:
+            to = partner
+            b = (me, owner(chip - 1), owner(chip + 1), owner(chip + 2))[kind - 3]
+        ref = place(i, l, b)
+        return pltpu.make_async_remote_copy(src_ref=ref, dst_ref=ref, send_sem=s_sem.at[kind, p], recv_sem=r_sem.at[kind, p],
+                                            device_id={"dp": to}, device_id_type=pl.DeviceIdType.MESH)
+    zero, one_ = [p for p, (i, l) in enumerate(pieces) if l == 0], [p for p, (i, l) in enumerate(pieces) if l == 1]
+    for a, b in zip(zero + one_, one_ + zero):
+        copy(0, a).start()
+        copy(1, b).start()
+    for p in range(len(pieces)):
+        copy(3, p).start()
+    for a, b in zip(zero, one_):
+        copy(0, a).wait_recv()
+        copy(2, a).start()
+        copy(4, a).start()
+        copy(1, b).wait_recv()
+        copy(2, b).start()
+        copy(5, b).start()
+    for a, b in zip(one_, zero):
+        copy(0, a).wait_recv()
+        copy(4, a).start()
+        copy(1, b).wait_recv()
+        copy(5, b).start()
+    for a, b in zip(zero, one_):
+        for p in (a, b):
+            copy(2, p).wait_recv()
+            copy(6, p).start()
+    for p in range(len(pieces)):
+        for kind in range(7):
+            copy(kind, p).wait_send()
+            if kind >= 3:
+                copy(kind, p).wait_recv()
+
+def gather(n, news):
+    dma = pltpu.SemaphoreType.DMA
+    full = [(w.shape[0], n * w.shape[1], w.shape[2]) for w in news]
+    return pl.pallas_call(
+        functools.partial(gather_kernel, n),
+        in_specs=[pl.BlockSpec(memory_space=pl.ANY)] * 3,
+        out_specs=[pl.BlockSpec(memory_space=pltpu.VMEM)] * 3,
+        out_shape=[pltpu.VMEM(s, BF16) for s in full],
+        scratch_shapes=[dma((6,)), dma((7, 6)), dma((7, 6))],
+        compiler_params=pltpu.CompilerParams(vmem_limit_bytes=1 << 20, collective_id=1, has_side_effects=True),
+        name="gather",
+    )(*news)
+
+def store_kernel(*refs):
+    half = (len(refs) - 1) // 2
+    copies = [pltpu.make_async_copy(refs[i], refs[half + i], refs[-1].at[i]) for i in range(half)]
+    for one in copies:
+        one.start()
+    for one in copies:
+        one.wait()
+
+def store(arrays):
+    k = len(arrays)
+    return pl.pallas_call(
+        store_kernel, in_specs=[pl.BlockSpec(memory_space=pltpu.VMEM)] * k, out_specs=[pl.BlockSpec(memory_space=pltpu.HBM)] * k,
+        out_shape=[pltpu.HBM(a.shape, a.dtype) for a in arrays], scratch_shapes=[pltpu.SemaphoreType.DMA((k,))],
+        compiler_params=pltpu.CompilerParams(vmem_limit_bytes=1 << 20), name="store")(*arrays)
 
 def solution(mesh):
     n = mesh.shape["dp"]
 
     def step(x, dy, wg, wu, wd, mg, mu, md, vg, vu, vd):
-        s, a, dh = tokens(x, dy, wg, wu, wd)
-
-        def grad(lhs, rhs):
-            term = lax.dot_general(lhs, rhs, (((0,), (0,)), ((), ())), preferred_element_type=F32).astype(BF16)
-            return lax.psum_scatter(term, "dp", scatter_dimension=0, tiled=True).astype(F32)
-
-        first, last = {}, {}
-        for to, l in ((last, 0), (first, 1)):
-            to["g"] = grad(a[l], s[3 * l])
-            to["u"] = grad(a[l], s[3 * l + 1])
-            to["d"] = grad(s[3 * l + 2], dh[l])
-        grads = [jnp.stack([first[k], last[k]]) for k in "gud"]
-        count = n * sum(g.size for g in grads)
-        total = lax.psum(sum(jnp.sum(g * g) for g in grads), "dp")
-        factor = jnp.minimum(1.0, 0.5 * lax.rsqrt(total / count + 1e-30))
-        me = lax.axis_index("dp")
-        new = []
-        for w, m, v, g in zip((wg, wu, wd), (mg, mu, md), (vg, vu, vd), grads):
-            rows = m.shape[1]
-            own = lax.dynamic_slice_in_dim(w, me * rows, rows, 1).astype(F32)
-            nw, nm, nv = adamw(own, m, v, g * factor)
-            new.append((lax.all_gather(nw, "dp", axis=1, tiled=True), nm, nv))
-        return tuple(one[i] for i in range(3) for one in new)
+        s, at, dh = tokens(x, dy, wg, wu, wd)
+        g, ss = grads(n, s, at, dh)
+        me = lax.axis_index("dp").astype(jnp.int32).reshape(1)
+        new, m, v = adam(n, me, ss, g, (wg, wu, wd), (mg, mu, md), (vg, vu, vd))
+        return (*store(gather(n, new)), *m, *v)
 
     data, whole, rows = P(("rep", "dp"), None, None), P(None, None, None), P(None, "dp", None)
     return jax.shard_map(step, mesh=mesh, in_specs=(data,) * 2 + (whole,) * 3 + (rows,) * 6,

time: 546 us -> 385 us (0.71); the launches traced: 539 us -> 385 us
  Pallas kernels: 113 us -> 375 us
  waiting for transfers between devices: 256 us -> 0 us
  matrix products: 90.4 us -> 0 us
  other arithmetic: 23.7 us -> 0 us
  between operations: 17.1 us -> 0.84 us
  blocking collectives: 15.9 us -> 0 us
  local copies, waits for them, and re-layouts: 21.8 us -> 8.57 us
    pallas_call x0 -> x4, Pallas kernels: none -> 261 us  [the longest x1 133 us: grads(): pl.pallas_call(functools.partial(grads_kernel, n), in_specs=[anyspec] * 3...]
    all_gather x3 -> x0, waiting for transfers between devices: 128 us -> none  [step(): new.append((lax.all_gather(nw, 'dp', axis=1, tiled=True), nm, nv))]
    reduce_scatter x6 -> x0, waiting for transfers between devices: 128 us -> none  [grad(): lax.psum_scatter(term, 'dp', scatter_dimension=0, tiled=True).astype(F32)]
    dot_general x6 -> x0, matrix products: 90.4 us -> none  [grad(): lax.dot_general(lhs, rhs, (((0,), (0,)), ((), ())), preferred_element_typ...]
    convert_element_type x3 -> x0, other arithmetic: 16.7 us -> none  [adamw(): return ((w - 0.02 * step).astype(BF16), m, v)]
    psum x1 -> x0, blocking collectives: 15.9 us -> none  [step(): total = lax.psum(sum((jnp.sum(g * g) for g in grads)), 'dp')]
    unnamed x11 -> x12, local copies, waits for them, and re-layouts: 21.8 us -> 8.57 us
    reduce_sum x3 -> x0, other arithmetic: 6.99 us -> none  [step(): total = lax.psum(sum((jnp.sum(g * g) for g in grads)), 'dp')]
  transfers between devices with their start and end apart: 9 -> 0, of which waited for: 7 -> 0; matrix products, arithmetic and copies ran while one was open for 17% -> 0% of each run, Pallas kernels for 0% -> 0%
where the time goes in v2:
time: 385 us
  Pallas kernels  375 us (97%)
  local copies, waits for them, and re-layouts  8.57 us (2%)
    pallas_call x1, Pallas kernels, grads(): pl.pallas_call(functools.partial(grads_kernel, n), in_specs=[anyspec] * 3...  133 us
    pallas_call x1, Pallas kernels, tokens(): pl.pallas_call(functools.partial(tokens_kernel, nf), grid=(t // tm,), in_...  114 us
    pallas_call x1, Pallas kernels, gather(): pl.pallas_call(functools.partial(gather_kernel, n), in_specs=[pl.BlockSpe...  109 us
    pallas_call x1, Pallas kernels, adam(): pl.pallas_call(functools.partial(adam_kernel, count), grid_spec=grid, out...  10.9 us
    pallas_call x1, Pallas kernels, store(): pl.pallas_call(store_kernel, in_specs=[pl.BlockSpec(memory_space=pltpu.VM...  8.58 us
    unnamed x12, local copies, waits for them, and re-layouts  8.57 us

profile of v2, /device:TPU:113, one launch (start us, length us, event | category | flops | bytes accessed | tf_op | source)
XLA Modules:
  0.0 384.7 jit_solution(6859697373839716255)
XLA Ops:
  0.6 114.3 %tokens.1 = (bf16[6,2048,2304]{2,1,0:T(8,128)(2,1)}, bf16[2,896,2048]{2,1,0:T(8,128)(2,1)}, bf16[2,2048,896]{2,1,0:T(8,128)(2,1)}) custom-call(bf16[1,2048,896]{2,1,0:T(8,128)(2,1)} %x_ref.1, bf16[1,2048,896]{2,1,0:T(8,128)(2,1)} %dy_ref.1, bf16[2,896,2304]{2,1,0:T(8,128)(2,1)} %refs_0_.1, bf16[2,896,2304]{2,1,0:T(8,128)(2,1)} %refs_1_.1, ...), custom_call_target="tpu_custom_call" | custom-call | tf_op jit(solution)/shard_map/tokens/pallas_call | solution.py:88
  114.9 132.6 %grads.1 = (bf16[18,672,128]{2,1,0:T(8,128)(2,1)}, f32[8,128]{1,0:T(8,128)}) custom-call(bf16[6,2048,2304]{2,1,0:T(8,128)(2,1)} %get-tuple-element.29.s_hbm, bf16[2,896,2048]{2,1,0:T(8,128)(2,1)} %get-tuple-element.30.at_hbm, bf16[2,2048,896]{2,1,0:T(8,128)(2,1)} %get-tuple-element.31.dh_hbm), custom_call_target="tpu_custom_call" | custom-call | tf_op jit(solution)/shard_map/grads/pallas_call | solution.py:271
  247.5 0.0 copy-start
  247.5 1.6 copy-done
  249.1 0.0 copy-start.1
  249.1 1.6 copy-done.1
  250.7 0.0 copy-start.2
  250.7 1.6 copy-done.2
  252.3 0.0 copy-start.3
  252.3 1.6 copy-done.3
  253.8 0.0 copy-start.4
  253.8 1.6 copy-done.4
  255.4 0.0 copy-start.5
  255.4 0.7 copy-done.5
  256.1 10.9 %adam.1 = (bf16[2,112,2304]{2,1,0:T(8,128)(2,1)S(1)}, bf16[2,112,2304]{2,1,0:T(8,128)(2,1)S(1)}, bf16[2,288,896]{2,1,0:T(8,128)(2,1)S(1)}, f32[2,112,2304]{2,1,0...) custom-call(s32[1]{0:T(128)} %bitcast.me_ref, ...), custom_call_target="tpu_custom_call" | custom-call | tf_op jit(solution)/shard_map/adam/pallas_call | solution.py:318
  267.0 108.9 %gather.1 = (bf16[2,896,2304]{2,1,0:T(8,128)(2,1)S(1)}, bf16[2,896,2304]{2,1,0:T(8,128)(2,1)S(1)}, bf16[2,2304,896]{2,1,0:T(8,128)(2,1)S(1)}) custom-call(bf16[2,112,2304]{2,1,0:T(8,128)(2,1)S(1)} %get-tuple-element.34.refs_0_, bf16[2,112,2304]{2,1,0:T(8,128)(2,1)S(1)} %get-tuple-element.35.refs_1_, bf16[2,288,896]{2,1,0:T(8,128)(2,1)S(1)} %get-tuple-element.36.refs_2_), custom_call_target="tpu_custom_call" | custom-call | tf_op jit(solution)/shard_map/gather/pallas_call | solution.py:391
  375.9 8.6 %store.1 = (bf16[2,896,2304]{2,1,0:T(8,128)(2,1)}, bf16[2,896,2304]{2,1,0:T(8,128)(2,1)}, bf16[2,2304,896]{2,1,0:T(8,128)(2,1)}) custom-call(bf16[2,896,2304]{2,1,0:T(8,128)(2,1)S(1)} %get-tuple-element.37.refs_0_, bf16[2,896,2304]{2,1,0:T(8,128)(2,1)S(1)} %get-tuple-element.38.refs_1_, bf16[2,2304,896]{2,1,0:T(8,128)(2,1)S(1)} %get-tuple-element.39.refs_2_), custom_call_target="tpu_custom_call" | custom-call | tf_op jit(solution)/shard_map/store/pallas_call | solution.py:411
Async XLA Ops:
  247.5 1.6 copy-start
  249.1 1.6 copy-start.1
  250.7 1.6 copy-start.2
  252.3 1.6 copy-start.3
  253.8 1.6 copy-start.4
  255.4 0.7 copy-start.5

commit v3 on v2

--- a/solution.py
+++ b/solution.py
@@ -98,6 +98,7 @@
 TN = (((0,), (0,)), ((), ()))
 NK = 3
 RING = 11
+L1, L2, L3 = 1, 3, 5
 
 def grads_kernel(n, s_hbm, at_hbm, dh_hbm, g_ref, ss_ref, at, dh, inb, st, re, sb, rt, cb, rf, ss, ssr,
                  in_sem, ld_sem, e_s, e_r, r1_s, r1_r, r2_s, r2_r, x_s, x_r):
@@ -149,20 +150,19 @@
 
         @pl.when(fresh)
         def _():
-            for one in loads(layer):
-                one.wait()
+            loads(layer)[0].wait()
+
+        @pl.when(lax.rem(c, 3 * NK) == 2 * NK)
+        def _():
+            loads(layer)[1].wait()
         slot = lax.rem(c, 2)
 
         @pl.when(kind < 2)
         def _():
-            def sub(j, _):
-                out = jnp.dot(at[...], inb[slot, :, pl.ds(pl.multiple_of(j * 256, 256), 256)], preferred_element_type=F32).astype(BF16)
-                for b in range(n):
-                    for i in range(2):
-                        st[lax.rem(core + b, 2), lax.rem(c, RING), b // 2, pl.ds(pl.multiple_of((2 * j + i) * rg, 16), rg), :] = \
-                            out[b * rg:(b + 1) * rg, i * 128:(i + 1) * 128]
-                return 0
-            lax.fori_loop(0, cw // 256, sub, 0)
+            out = jnp.dot(at[...], inb[slot], preferred_element_type=F32).astype(BF16)
+            for b in range(n):
+                for i in range(cw // 128):
+                    st[lax.rem(core + b, 2), lax.rem(c, RING), b // 2, i * rg:(i + 1) * rg, :] = out[b * rg:(b + 1) * rg, i * 128:(i + 1) * 128]
 
         @pl.when(kind == 2)
         def _():
@@ -203,9 +203,9 @@
             return jnp.minimum(u + 1 + ahead, chunks)
         lax.fori_loop(jnp.where(s == 0, 0, done(s - 1)), done(s), compute, 0)
 
-        @pl.when((s >= 2) & (s < chunks + 2))
-        def _():
-            c = s - 2
+        @pl.when((s >= L1) & (s < chunks + L1))
+        def _():
+            c = s - L1
             exchange(c).wait()
             r = lax.rem(c, 3)
             sb[r, 0] = pair(c, far, A).astype(BF16)
@@ -213,9 +213,9 @@
             sb[r, 2] = pair(c, prv, B).astype(BF16)
             sb[r, 3] = pair(c, nxt, A).astype(BF16)
 
-        @pl.when((s >= 4) & (s < chunks + 4))
-        def _():
-            c = s - 4
+        @pl.when((s >= L2) & (s < chunks + L2))
+        def _():
+            c = s - L2
             for i, one in enumerate(first(c)):
                 one.wait_send()
                 if i < 2:
@@ -228,19 +228,19 @@
         def _():
             exchange(s).start()
 
-        @pl.when((s >= 4) & (s < chunks + 4))
-        def _():
-            for one in second(s - 4):
+        @pl.when((s >= L2) & (s < chunks + L2))
+        def _():
+            for one in second(s - L2):
                 one.start()
 
-        @pl.when((s >= 2) & (s < chunks + 2))
-        def _():
-            for one in first(s - 2):
+        @pl.when((s >= L1) & (s < chunks + L1))
+        def _():
+            for one in first(s - L1):
                 one.start()
 
-        @pl.when(s >= 6)
-        def _():
-            c = s - 6
+        @pl.when(s >= L3)
+        def _():
+            c = s - L3
             for one in first(c)[2:]:
                 one.wait_recv()
             for one in second(c):
@@ -251,7 +251,7 @@
             ss[...] += jnp.sum((wide * wide).reshape(rows // 8, 8, 128), 0)
         return 0
 
-    lax.fori_loop(0, chunks + 6, step, 0)
+    lax.fori_loop(0, chunks + L3, step, 0)
     tell = [remote(ss, ssr.at[o], x_s.at[o], x_r.at[o], lax.rem(me + o, n)) for o in range(1, n)]
     for one in tell:
         one.start()
@@ -272,7 +272,7 @@
         functools.partial(grads_kernel, n),
         in_specs=[anyspec] * 3,
         out_specs=[pl.BlockSpec(memory_space=pltpu.VMEM)] * 2,
-        out_shape=[jax.ShapeDtypeStruct((chunks, rows, 128), BF16), jax.ShapeDtypeStruct((8, 128), F32)],
+        out_shape=[pltpu.VMEM((chunks, rows, 128), BF16), pltpu.VMEM((8, 128), F32)],
         scratch_shapes=[pltpu.VMEM((d, t), BF16), pltpu.VMEM((t, d), BF16), pltpu.VMEM((2, t, ff // NK), BF16),
                         pltpu.VMEM((2, RING, n // 2, rows, 128), BF16), pltpu.VMEM((chunks, n // 2, rows, 128), BF16),
                         pltpu.VMEM((3, 4, half, 128), BF16), pltpu.VMEM((chunks, 2, half, 128), BF16),
@@ -280,77 +280,74 @@
                         pltpu.VMEM((8, 128), F32), pltpu.VMEM((n, 8, 128), F32),
                         dma((2,)), dma((2,)), dma((4,)), dma((chunks,)), dma((4, 4)), dma((chunks, 4)), dma((4, 2)), dma((chunks, 2)),
                         dma((n,)), dma((n,))],
-        compiler_params=pltpu.CompilerParams(vmem_limit_bytes=67043328, collective_id=0, has_side_effects=True),
+        compiler_params=pltpu.CompilerParams(vmem_limit_bytes=58 << 20, collective_id=0, has_side_effects=True),
         name="grads",
     )(s, at, dh)
 
-def adam_kernel(count, me_ref, ss_ref, g_ref, *refs):
-    ws, ms, vs, outs = refs[:3], refs[3:6], refs[6:9], refs[9:]
-    total = jnp.sum(ss_ref[...], keepdims=True)
-    factor = jnp.minimum(1.0, 0.5 * lax.rsqrt(total / count + 1e-30))
-    for i in range(3):
-        rows, cols = ms[i].shape[1:]
-        for t in range(cols // 128):
-            c = slice(t * 128, (t + 1) * 128)
-            g = g_ref[0, i, 0, t * rows:(t + 1) * rows, :].astype(F32) * factor
-            m = 0.9 * ms[i][0, :, c] + 0.1 * g
-            v = 0.95 * vs[i][0, :, c] + 0.05 * g * g
-            w = ws[i][0, :, c].astype(F32)
-            outs[i][0, :, c] = (w - 0.02 * (m * lax.rsqrt(v + 1e-8) + 0.1 * w)).astype(BF16)
-            outs[3 + i][0, :, c] = m
-            outs[6 + i][0, :, c] = v
-
-def adam(n, me, ss, g, ws, ms, vs):
-    layers, d, ff = ws[0].shape
-    rg, rk, cw = d // n, ff // n // NK, ff // NK
-    wide = lambda at: pl.BlockSpec((1, rg, cw), lambda l, k, me: (l, at(me), k))
-    tall = lambda at: pl.BlockSpec((1, rk, d), lambda l, k, me: (l, NK * at(me) + k, 0))
-    none, mine = (lambda me: 0), (lambda me: me[0])
-    three = lambda at: [wide(at), wide(at), tall(at)]
-    shapes = lambda dt: [jax.ShapeDtypeStruct(m.shape, dt) for m in ms]
-    grid = pltpu.PrefetchScalarGridSpec(
-        num_scalar_prefetch=1, grid=(layers, NK),
-        in_specs=[pl.BlockSpec((8, 128), lambda l, k, me: (0, 0)),
-                  pl.BlockSpec((1, 3, 1) + g.shape[1:], lambda l, k, me: (layers - 1 - l, 0, k, 0, 0))]
-        + three(mine) + three(none) * 2,
-        out_specs=three(none) * 3)
-    count = n * sum(m.size for m in ms)
-    out = pl.pallas_call(functools.partial(adam_kernel, count), grid_spec=grid, out_shape=shapes(BF16) + shapes(F32) * 2,
-                         compiler_params=pltpu.CompilerParams(vmem_limit_bytes=40 << 20), name="adam",
-                         )(me, ss, g.reshape((layers, 3, NK) + g.shape[1:]), *ws, *ms, *vs)
-    return out[:3], out[3:6], out[6:]
-
-def gather_kernel(n, *refs):
-    mine, outs, (in_sem, s_sem, r_sem) = refs[:3], refs[3:6], refs[6:]
+
+def update_kernel(n, count, ss_ref, g_ref, *refs):
+    given, outs, (in_sem, s_sem, r_sem) = refs[:9], refs[9:18], refs[18:]
     me = lax.axis_index("dp")
     chips = n // 2
     core, chip = lax.rem(me, 2), lax.div(me, 2)
     owner = lambda c, q=None: lax.rem(c + chips, chips) * 2 + (core if q is None else q)
     right, left, partner = owner(chip + 1), owner(chip - 1), owner(chip, 1 - core)
-    pieces = [(i, l) for l in range(2) for i in range(3)]
+    pieces = [(i, l) for i in range(3) for l in range(2)]
+
+    def rows_of(i, b, k=0, part=1):
+        rows = outs[3 + i].shape[1]
+        return pl.ds(pl.multiple_of(b * rows + k * (rows // part), 16), rows // part)
 
     def place(i, l, b):
-        rows = mine[i].shape[1]
-        return outs[i].at[l, pl.ds(pl.multiple_of(b * rows, 16), rows), :]
-    own = [pltpu.make_async_copy(mine[i].at[l], place(i, l, me), in_sem.at[p]) for p, (i, l) in enumerate(pieces)]
-    for one in own:
-        one.start()
+        return outs[i].at[l, rows_of(i, b), :]
+
+    def arrive(p):
+        i, l = pieces[p]
+        return (pltpu.make_async_copy(given[i].at[l, rows_of(i, me), :], place(i, l, me), in_sem.at[0, p]),
+                pltpu.make_async_copy(given[3 + i].at[l], outs[3 + i].at[l], in_sem.at[1, p]),
+                pltpu.make_async_copy(given[6 + i].at[l], outs[6 + i].at[l], in_sem.at[2, p]))
+    for p in range(len(pieces)):
+        for one in arrive(p):
+            one.start()
     barrier = pltpu.get_barrier_semaphore()
     for to in (left, right, partner):
         pl.semaphore_signal(barrier, inc=1, device_id={"dp": to}, device_id_type=pl.DeviceIdType.MESH)
-    pl.semaphore_wait(barrier, 3)
-    for one in own:
-        one.wait()
-
-    def copy(kind, p, there=False):
+    total = jnp.sum(ss_ref[...], keepdims=True)
+    factor = jnp.minimum(1.0, 0.5 * lax.rsqrt(total / count + 1e-30))
+
+    def renew(p):
         i, l = pieces[p]
-        far_right = l == 0
+        for one in arrive(p):
+            one.wait()
+        full, cols = outs[3 + i].shape[1:]
+        rows, tiles = (full, cols // NK // 128) if i < 2 else (full // NK, cols // 128)
+
+        def part(k, _):
+            for t in range(tiles):
+                if i < 2:
+                    r, own = pl.ds(0, full), rows_of(i, me)
+                    c = pl.ds(pl.multiple_of(k * (cols // NK) + t * 128, 128), 128)
+                else:
+                    r, own = pl.ds(pl.multiple_of(k * rows, 16), rows), rows_of(i, me, k, NK)
+                    c = pl.ds(t * 128, 128)
+                g = g_ref[(1 - l) * 3 * NK + i * NK + k, t * rows:(t + 1) * rows, :].astype(F32) * factor
+                m = 0.9 * outs[3 + i][l, r, c] + 0.1 * g
+                v = 0.95 * outs[6 + i][l, r, c] + 0.05 * g * g
+                w = outs[i][l, own, c].astype(F32)
+                outs[i][l, own, c] = (w - 0.02 * (m * lax.rsqrt(v + 1e-8) + 0.1 * w)).astype(BF16)
+                outs[3 + i][l, r, c] = m
+                outs[6 + i][l, r, c] = v
+            return 0
+        lax.fori_loop(0, NK, part, 0)
+
+    def copy(kind, p):
+        i, l = pieces[p]
         if kind == 0:
             to, b = right, me
         elif kind == 1:
             to, b = left, me
         elif kind == 2:
-            to, b = (right, owner(chip - 1)) if far_right else (left, owner(chip + 1))
+            to, b = (right, owner(chip - 1)) if l == 0 else (left, owner(chip + 1))
         else:
             to = partner
             b = (me, owner(chip - 1), owner(chip + 1), owner(chip + 2))[kind - 3]
@@ -358,9 +355,16 @@
         return pltpu.make_async_remote_copy(src_ref=ref, dst_ref=ref, send_sem=s_sem.at[kind, p], recv_sem=r_sem.at[kind, p],
                                             device_id={"dp": to}, device_id_type=pl.DeviceIdType.MESH)
     zero, one_ = [p for p, (i, l) in enumerate(pieces) if l == 0], [p for p, (i, l) in enumerate(pieces) if l == 1]
-    for a, b in zip(zero + one_, one_ + zero):
-        copy(0, a).start()
-        copy(1, b).start()
+    for p in range(len(pieces)):
+        renew(p)
+        if p == 0:
+            pl.semaphore_wait(barrier, 3)
+        if p > 0:
+            copy(0 if pieces[p - 1][1] == 0 else 1, p - 1).start()
+    copy(1, len(pieces) - 1).start()
+    for a, b in zip(zero, one_):
+        copy(0, b).start()
+        copy(1, a).start()
     for p in range(len(pieces)):
         copy(3, p).start()
     for a, b in zip(zero, one_):
@@ -385,18 +389,19 @@
             if kind >= 3:
                 copy(kind, p).wait_recv()
 
-def gather(n, news):
-    dma = pltpu.SemaphoreType.DMA
-    full = [(w.shape[0], n * w.shape[1], w.shape[2]) for w in news]
-    return pl.pallas_call(
-        functools.partial(gather_kernel, n),
-        in_specs=[pl.BlockSpec(memory_space=pl.ANY)] * 3,
-        out_specs=[pl.BlockSpec(memory_space=pltpu.VMEM)] * 3,
-        out_shape=[pltpu.VMEM(s, BF16) for s in full],
-        scratch_shapes=[dma((6,)), dma((7, 6)), dma((7, 6))],
-        compiler_params=pltpu.CompilerParams(vmem_limit_bytes=1 << 20, collective_id=1, has_side_effects=True),
-        name="gather",
-    )(*news)
+def update(n, ss, g, ws, ms, vs):
+    dma, vmem = pltpu.SemaphoreType.DMA, pl.BlockSpec(memory_space=pltpu.VMEM)
+    count = n * sum(m.size for m in ms)
+    out = pl.pallas_call(
+        functools.partial(update_kernel, n, count),
+        in_specs=[vmem] * 2 + [pl.BlockSpec(memory_space=pltpu.HBM)] * 9,
+        out_specs=[vmem] * 9,
+        out_shape=[pltpu.VMEM(a.shape, a.dtype) for a in (*ws, *ms, *vs)],
+        scratch_shapes=[dma((3, 6)), dma((7, 6)), dma((7, 6))],
+        compiler_params=pltpu.CompilerParams(vmem_limit_bytes=8 << 20, collective_id=1, has_side_effects=True),
+        name="update",
+    )(ss, g, *(pltpu.with_memory_space_constraint(a, pltpu.HBM) for a in (*ws, *ms, *vs)))
+    return out
 
 def store_kernel(*refs):
     half = (len(refs) - 1) // 2
@@ -419,9 +424,7 @@
     def step(x, dy, wg, wu, wd, mg, mu, md, vg, vu, vd):
         s, at, dh = tokens(x, dy, wg, wu, wd)
         g, ss = grads(n, s, at, dh)
-        me = lax.axis_index("dp").astype(jnp.int32).reshape(1)
-        new, m, v = adam(n, me, ss, g, (wg, wu, wd), (mg, mu, md), (vg, vu, vd))
-        return (*store(gather(n, new)), *m, *v)
+        return tuple(store(update(n, ss, g, (wg, wu, wd), (mg, mu, md), (vg, vu, vd))))
 
     data, whole, rows = P(("rep", "dp"), None, None), P(None, None, None), P(None, "dp", None)
     return jax.shard_map(step, mesh=mesh, in_specs=(data,) * 2 + (whole,) * 3 + (rows,) * 6,

time: 385 us -> 361 us (0.938)
  Pallas kernels: 375 us -> 356 us
  local copies, waits for them, and re-layouts: 8.57 us -> 3.52 us
    pallas_call x1, Pallas kernels: 133 us -> 121 us  [grads(): pl.pallas_call(functools.partial(grads_kernel, n), in_specs=[anyspec] * 3...]
    pallas_call x2 -> x1, Pallas kernels: 120 us -> 109 us  [update(): pl.pallas_call(functools.partial(update_kernel, n, count), in_specs=[vmem...]
    unnamed x12 -> x4, local copies, waits for them, and re-layouts: 8.57 us -> 3.52 us
where the time goes in v3:
time: 361 us; the launch traced here: 360 us
  Pallas kernels  356 us (99%)
    pallas_call x1, Pallas kernels, grads(): pl.pallas_call(functools.partial(grads_kernel, n), in_specs=[anyspec] * 3...  121 us
    pallas_call x1, Pallas kernels, tokens(): pl.pallas_call(functools.partial(tokens_kernel, nf), grid=(t // tm,), in_...  114 us
    pallas_call x1, Pallas kernels, update(): pl.pallas_call(functools.partial(update_kernel, n, count), in_specs=[vmem...  109 us
    pallas_call x1, Pallas kernels, store(): pl.pallas_call(store_kernel, in_specs=[pl.BlockSpec(memory_space=pltpu.VM...  12.2 us

profile of v3, /device:TPU:113, one launch (start us, length us, event | category | flops | bytes accessed | tf_op | source)
XLA Modules:
  0.0 360.4 jit_solution(5058504784587623048)
XLA Ops:
  0.6 114.3 %tokens.1 = (bf16[6,2048,2304]{2,1,0:T(8,128)(2,1)}, bf16[2,896,2048]{2,1,0:T(8,128)(2,1)}, bf16[2,2048,896]{2,1,0:T(8,128)(2,1)}) custom-call(bf16[1,2048,896]{2,1,0:T(8,128)(2,1)} %x_ref.1, bf16[1,2048,896]{2,1,0:T(8,128)(2,1)} %dy_ref.1, bf16[2,896,2304]{2,1,0:T(8,128)(2,1)} %refs_0_.1, bf16[2,896,2304]{2,1,0:T(8,128)(2,1)} %refs_1_.1, ...), custom_call_target="tpu_custom_call" | custom-call | tf_op jit(solution)/shard_map/tokens/pallas_call | solution.py:88
  114.9 121.0 %grads.1 = (bf16[18,672,128]{2,1,0:T(8,128)(2,1)S(1)}, f32[8,128]{1,0:T(8,128)S(1)}) custom-call(bf16[6,2048,2304]{2,1,0:T(8,128)(2,1)} %get-tuple-element.23.s_hbm, bf16[2,896,2048]{2,1,0:T(8,128)(2,1)} %get-tuple-element.24.at_hbm, bf16[2,2048,896]{2,1,0:T(8,128)(2,1)} %get-tuple-element.25.dh_hbm), custom_call_target="tpu_custom_call" | custom-call | tf_op jit(solution)/shard_map/grads/pallas_call | solution.py:271
  235.9 0.0 copy-start
  235.9 1.6 copy-done
  237.6 0.0 copy-start.1
  237.6 1.9 copy-done.1
  239.4 108.6 %update.1 = (bf16[2,896,2304]{2,1,0:T(8,128)(2,1)S(1)}, bf16[2,896,2304]{2,1,0:T(8,128)(2,1)S(1)}, bf16[2,2304,896]{2,1,0:T(8,128)(2,1)S(1)}, f32[2,112,2304]{2,...) custom-call(f32[8,128]{1,0:T(8,128)S(1)} %get-tuple-element.26.ss_re, ...), custom_call_target="tpu_custom_call" | custom-call | tf_op jit(solution)/shard_map/update/pallas_call | solution.py:395
  348.0 12.2 %store.1 = (bf16[2,896,2304]{2,1,0:T(8,128)(2,1)}, bf16[2,896,2304]{2,1,0:T(8,128)(2,1)}, bf16[2,2304,896]{2,1,0:T(8,128)(2,1)}, f32[2,112,2304]{2,1,0:T(8,128)}...) custom-call(bf16[2,896,2304]{2,1,0:T(8,128)(2,1)S(1)} %get-tuple-ele, ...), custom_call_target="tpu_custom_call" | custom-call | tf_op jit(solution)/shard_map/store/pallas_call | solution.py:416
Async XLA Ops:
  235.9 1.7 copy-start
  237.6 1.9 copy-start.1

commit v4 on v3

v4 whole, which is shorter than its diff:
```python
import functools

import jax
import jax.numpy as jnp
from jax import lax
from jax.experimental import pallas as pl
from jax.experimental.pallas import tpu as pltpu
from jax.sharding import PartitionSpec as P

F32, BF16 = jnp.float32, jnp.bfloat16
NT = (((1,), (1,)), ((), ()))

def dot(a, b):
    return jnp.dot(a, b, preferred_element_type=F32)
def dot_t(a, b):
    return lax.dot_general(a, b, NT, preferred_element_type=F32)

def norm_of(h):
    wide = h.astype(F32)
    scale = lax.rsqrt(jnp.mean(wide * wide, -1, keepdims=True) + 1e-6)
    return wide, scale

def sigmoid(g):
    return 0.5 * jnp.tanh(0.5 * g) + 0.5

def swiglu_back(dp, g, u):
    sig = sigmoid(g)
    si = g * sig
    return (dp * u * (sig + si - si * sig)).astype(BF16), (dp * si).astype(BF16), (si * u).astype(BF16)

def tokens_kernel(nf, x_ref, dy_ref, wg_hbm, wu_hbm, wd_hbm, s_ref, gu_ref, at_ref, h_ref, wg, wu, wd, sems):
    i = pl.program_id(0)
    ff = wg.shape[2]
    fb = ff // nf
    cols = [slice(k * fb, (k + 1) * fb) for k in range(nf)]
    copies = {(l, j): pltpu.make_async_copy(h.at[l], v.at[l], sems.at[l, j])
              for l in range(2) for j, (h, v) in enumerate(((wg_hbm, wg), (wu_hbm, wu), (wd_hbm, wd)))}

    @pl.when(i == 0)
    def _():
        for one in copies.values():
            one.start()

    def arrive(*which):
        @pl.when(i == 0)
        def _():
            for one in which:
                copies[one].wait()

    x = x_ref[0]
    wide, scale = norm_of(x)
    a0 = (wide * scale).astype(BF16)
    at_ref[1] = a0.T
    arrive((0, 0), (0, 1), (0, 2))
    down = None
    for c in cols:
        g, u = dot(a0, wg[0, :, c]), dot(a0, wu[0, :, c])
        gu_ref[0, :, c] = g
        gu_ref[1, :, c] = u
        p = (g * sigmoid(g) * u).astype(BF16)
        s_ref[3, :, c] = p
        d = dot(p, wd[0, c, :])
        down = d if down is None else down + d
    h1 = x + down.astype(BF16)
    h_ref[...] = h1
    wide, scale = norm_of(h1)
    a1 = (wide * scale).astype(BF16)
    at_ref[0] = a1.T
    dy = dy_ref[0]
    arrive((1, 0), (1, 1), (1, 2))
    for c in cols:
        g, u = dot(a1, wg[1, :, c]), dot(a1, wu[1, :, c])
        dp = dot_t(dy, wd[1, c, :]).astype(BF16).astype(F32)
        s_ref[0, :, c], s_ref[1, :, c], s_ref[2, :, c] = swiglu_back(dp, g, u)

def tokens(x, dy, wg, wu, wd, tm=256, nf=3):
    _, t, d = x.shape
    ff = wg.shape[2]
    tile = pl.BlockSpec((1, tm, d), lambda i: (0, i, 0))
    anyspec = pl.BlockSpec(memory_space=pl.ANY)
    wide = lambda k: pl.BlockSpec((k, tm, ff), lambda i: (0, i, 0))
    return pl.pallas_call(
        functools.partial(tokens_kernel, nf), grid=(t // tm,),
        in_specs=[tile, tile, anyspec, anyspec, anyspec],
        out_specs=[wide(4), wide(2), pl.BlockSpec((2, d, tm), lambda i: (0, 0, i)), pl.BlockSpec((tm, d), lambda i: (i, 0))],
        out_shape=[jax.ShapeDtypeStruct((4, t, ff), BF16), jax.ShapeDtypeStruct((2, t, ff), F32),
                   jax.ShapeDtypeStruct((2, d, t), BF16), jax.ShapeDtypeStruct((t, d), BF16)],
        scratch_shapes=[pltpu.VMEM(wg.shape, BF16), pltpu.VMEM(wu.shape, BF16), pltpu.VMEM(wd.shape, BF16), pltpu.SemaphoreType.DMA((2, 3))],
        compiler_params=pltpu.CompilerParams(vmem_limit_bytes=67043328, dimension_semantics=("arbitrary",)),
        name="tokens",
    )(x, dy, wg, wu, wd)

TN = (((0,), (0,)), ((), ()))
NK, RING, AHEAD = 3, 9, 5
L1, L2, L3 = 1, 3, 5
WHEN = (*range(6), 5, 6, *range(6, 12), 11, *range(11, 18))
SEND = (*range(9), 11, *range(11, 13), *range(12, 18))
PENDING = 6

def grads_kernel(n, s_hbm, gu_hbm, at_hbm, h_hbm, dy_hbm, wg_hbm, wu_hbm, wd_hbm, g_ref, ss_ref,
                 at, dh, inb, w1, wdb, gub, hb, gout, st, re, sb, rt, cb, rf, ss, ssr,
                 in_sem, ld_sem, gu_sem, b_sem, g_sem, e_s, e_r, r1_s, r1_r, r2_s, r2_r, x_s, x_r, free):
    me = lax.axis_index("dp")
    core, chip = lax.rem(me, 2), lax.div(me, 2)
    chips = n // 2
    t, d = dh.shape
    ff = wg_hbm.shape[2]
    chunks, rows = g_ref.shape[:2]
    slots = chunks // 2
    cw, rg, rk = ff // NK, d // n, ff // n // NK
    half = rows // 2
    A, B = pl.ds(0, half), pl.ds(half, half)
    nxt, prv, far = lax.rem(chip + 1, chips), lax.rem(chip + chips - 1, chips), lax.rem(chip + 2, chips)
    right, left, partner = nxt * 2 + core, prv * 2 + core, chip * 2 + (1 - core)

    def remote(src, dst, send, recv, to):
        return pltpu.make_async_remote_copy(src_ref=src, dst_ref=dst, send_sem=send, recv_sem=recv,
                                            device_id={"dp": to}, device_id_type=pl.DeviceIdType.MESH)

    def fetch(c):
        return pltpu.make_async_copy(s_hbm.at[lax.div(c, NK), :, pl.ds(pl.multiple_of(lax.rem(c, NK) * cw, cw), cw)],
                                     inb.at[lax.rem(c, 2)], in_sem.at[lax.rem(c, 2)])

    def down(k):
        return pltpu.make_async_copy(wd_hbm.at[0, pl.ds(pl.multiple_of(k * cw, cw), cw), :], wdb, ld_sem.at[2])

    quarter = t // 4

    def saved(q, one):
        return pltpu.make_async_copy(
            gu_hbm.at[one, pl.ds(pl.multiple_of(lax.rem(q, 4) * quarter, quarter), quarter), pl.ds(pl.multiple_of(lax.div(q, 4) * cw, cw), cw)],
            gub.at[lax.rem(q, 2), one], gu_sem.at[one, lax.rem(q, 2)])

    def cotangent(q, one):
        return [pltpu.make_async_copy(s_hbm.at[one, pl.ds(pl.multiple_of(q * quarter, quarter), quarter), pl.ds(k * cw, cw)],
                                      inb.at[one, pl.ds(k * quarter, quarter), :], b_sem.at[one, k]) for k in range(NK)]

    def state(q):
        return pltpu.make_async_copy(h_hbm.at[pl.ds(pl.multiple_of(q * quarter, quarter), quarter), :], hb, b_sem.at[2, 0])

    w1_load = [pltpu.make_async_copy(w.at[1], w1.at[one], b_sem.at[2, 1 + one]) for one, w in enumerate((wg_hbm, wu_hbm))]
    at_load = [pltpu.make_async_copy(at_hbm.at[l], at, ld_sem.at[0]) for l in range(2)]
    dy_load = pltpu.make_async_copy(dy_hbm.at[0], dh, ld_sem.at[1])
    at_load[0].start()
    fetch(0).start()
    barrier = pltpu.get_barrier_semaphore()
    for o in range(1, n):
        pl.semaphore_signal(barrier, inc=1, device_id={"dp": lax.rem(me + o, n)}, device_id_type=pl.DeviceIdType.MESH)
    pl.semaphore_wait(barrier, n - 1)
    ss[...] = jnp.zeros_like(ss)

    def place(other, c):
        return (1 - other) * lax.rem(c, RING) + other * (RING + lax.rem(c, AHEAD))

    def back_through_norm(q):
        @pl.when(q == 0)
        def _():
            for one in (*cotangent(0, 0), *cotangent(0, 1), state(0)):
                one.start()
            for one in w1_load:
                one.wait()
        parts = []
        for one in range(2):
            for copy in cotangent(q, one):
                copy.wait()
            total = sum(dot_t(inb[one, k * quarter:(k + 1) * quarter, :], w1[one, :, k * cw:(k + 1) * cw]) for k in range(NK))
            parts.append(total.astype(BF16))

            @pl.when(q < 3)
            def _():
                for copy in cotangent(q + 1, one):
                    copy.start()
        state(q).wait()
        r = pl.ds(pl.multiple_of(q * quarter, quarter), quarter)
        wide, scale = norm_of(hb[...])
        da = (parts[0] + parts[1]).astype(F32)
        coef = jnp.sum(da * wide, -1, keepdims=True) * (scale * scale * scale) * (-1.0 / d)
        dh[r, :] = dh[r, :] + (da * scale + wide * coef).astype(BF16)

        @pl.when(q < 3)
        def _():
            state(q + 1).start()

        @pl.when(q == 3)
        def _():
            fetch(3 * NK).start()
            down(0).start()
            for one in range(2):
                saved(0, one).start()

    def back_to_hidden(k):
        down(k).wait()

        def tile(j, _):
            q = 4 * k + j
            for one in range(2):
                saved(q, one).wait()

            @pl.when(q < 4 * NK - 1)
            def _():
                for one in range(2):
                    saved(q + 1, one).start()
            r = pl.ds(pl.multiple_of(j * quarter, quarter), quarter)
            for p in range(NK):
                part = slice(p * (cw // NK), (p + 1) * (cw // NK))
                dp = dot_t(dh[r, :], wdb[part, :]).astype(BF16).astype(F32)
                inb[0, r, part], inb[1, r, part], _ = swiglu_back(dp, gub[lax.rem(q, 2), 0, :, part], gub[lax.rem(q, 2), 1, :, part])
            return 0
        lax.fori_loop(0, 4, tile, 0)

        @pl.when(k < NK - 1)
        def _():
            down(k + 1).start()

    def compute(item, _):
        first, last = item < 3 * NK, item >= 3 * NK + 4

        @pl.when(first | last)
        def _():
            chunk(jnp.where(first, item, item - 4))

        @pl.when((item >= 3 * NK) & (item < 3 * NK + 4))
        def _():
            back_through_norm(item - 3 * NK)
        return 0

    def chunk(c):
        k, slot = lax.rem(c, NK), lax.rem(c, 2)
        wide_kind = (c < 2 * NK) | (c >= 4 * NK)

        @pl.when(c == 0)
        def _():
            at_load[0].wait()
            dy_load.start()

        @pl.when(c == 1)
        def _():
            for one in w1_load:
                one.start()

        @pl.when(c == 2 * NK)
        def _():
            dy_load.wait()
            at_load[1].start()

        @pl.when(c == 4 * NK)
        def _():
            at_load[1].wait()

        @pl.when(c < 4 * NK)
        def _():
            fetch(c).wait()

        @pl.when((c + 1 < 4 * NK) & (c + 1 != 3 * NK))
        def _():
            fetch(c + 1).start()

        @pl.when((c >= 4 * NK) & (slot == 0))
        def _():
            back_to_hidden(lax.div(c - 4 * NK, 2))

        @pl.when(wide_kind)
        def _():
            out = dot(at[...], inb[slot]).astype(BF16)
            for b in range(n):
                for i in range(cw // 128):
                    st[place(lax.rem(core + b, 2), c), b // 2, i * rg:(i + 1) * rg, :] = out[b * rg:(b + 1) * rg, i * 128:(i + 1) * 128]

        @pl.when((c >= 2 * NK) & (c < 4 * NK))
        def _():
            def sub(j, _):
                wide = cw // 2
                out = lax.dot_general(inb[slot, :, pl.ds(pl.multiple_of(j * wide, 128), wide)], dh[...], TN, preferred_element_type=F32).astype(BF16)
                for i in range(wide // rk):
                    q = (2 * k + j) * (wide // rk) + i
                    b, part = lax.div(q, NK), lax.rem(q, NK)
                    for tile in range(d // 128):
                        st[place(lax.rem(core + b, 2), c - k + part), lax.div(b, 2), tile * rk:(tile + 1) * rk, :] = \
                            out[i * rk:(i + 1) * rk, tile * 128:(tile + 1) * 128]
                return 0
            lax.fori_loop(0, 2, sub, 0)

    def exchange(c):
        return remote(st.at[place(1, c)], re.at[lax.rem(c, slots)], e_s.at[lax.rem(c, PENDING)], e_r.at[c], partner)

    def first(c):
        r, q, v = lax.rem(c, PENDING), lax.rem(c, PENDING), lax.rem(c, slots)
        return (remote(sb.at[r, 0], rt.at[v, 0], r1_s.at[q, 0], r1_r.at[c, 0], left),
                remote(sb.at[r, 1], rt.at[v, 1], r1_s.at[q, 1], r1_r.at[c, 1], right),
                remote(sb.at[r, 2], rf.at[v, 0, B], r1_s.at[q, 2], r1_r.at[c, 2], left),
                remote(sb.at[r, 3], rf.at[v, 1, A], r1_s.at[q, 3], r1_r.at[c, 3], right))

    def second(c):
        r, q, v = lax.rem(c, PENDING), lax.rem(c, PENDING), lax.rem(c, slots)
        return (remote(cb.at[r, 0], rf.at[v, 0, A], r2_s.at[q, 0], r2_r.at[c, 0], left),
                remote(cb.at[r, 1], rf.at[v, 1, B], r2_s.at[q, 1], r2_r.at[c, 1], right))

    def keep(c):
        return pltpu.make_async_copy(gout.at[lax.rem(c, 2)], g_ref.at[c], g_sem.at[lax.rem(c, 2)])

    def pair(c, to, part):
        return st[place(0, c), to, part, :].astype(F32) + re[lax.rem(c, slots), to, part, :].astype(F32)

    def step(s, _):
        def done(u):
            return sum(jnp.where(u >= at_, 1, 0) for at_ in WHEN)

        def sent(u):
            return sum(jnp.where(u >= at_, 1, 0) for at_ in SEND)

        def each(lag):
            def run(stage):
                def one(c, _):
                    stage(c)
                    return 0
                lax.fori_loop(sent(s - lag - 1), sent(s - lag), one, 0)
            return run

        lax.fori_loop(jnp.where(s == 0, 0, done(s - 1)), done(s), compute, 0)

        @each(L1)
        def _(c):
            exchange(c).wait()
            r = lax.rem(c, PENDING)
            sb[r, 0] = pair(c, far, A).astype(BF16)
            sb[r, 1] = pair(c, far, B).astype(BF16)
            sb[r, 2] = pair(c, prv, B).astype(BF16)
            sb[r, 3] = pair(c, nxt, A).astype(BF16)

        @each(L2)
        def _(c):
            for i, one in enumerate(first(c)):
                one.wait_send()
                if i < 2:
                    one.wait_recv()
            r = lax.rem(c, PENDING)
            cb[r, 0] = (pair(c, prv, A) + rt[lax.rem(c, slots), 0].astype(F32)).astype(BF16)
            cb[r, 1] = (pair(c, nxt, B) + rt[lax.rem(c, slots), 1].astype(F32)).astype(BF16)

        @each(0)
        def _(c):

            @pl.when(c >= slots)
            def _():
                pl.semaphore_wait(free.at[0], 1)
            exchange(c).start()

        @each(L2)
        def _(c):
            for one in second(c):
                one.start()

        @each(L1)
        def _(c):

            @pl.when(c >= slots)
            def _():
                pl.semaphore_wait(free.at[1], 1)
                pl.semaphore_wait(free.at[2], 1)
            for one in first(c):
                one.start()

        @each(L3)
        def _(c):
            for one in first(c)[2:]:
                one.wait_recv()
            for one in second(c):
                one.wait()
            g = (pair(c, chip, pl.ds(0, rows)) + rf[lax.rem(c, slots), 0].astype(F32) + rf[lax.rem(c, slots), 1].astype(F32)).astype(BF16)
            @pl.when(c >= 2)
            def _():
                keep(c - 2).wait()
            gout[lax.rem(c, 2)] = g
            keep(c).start()
            wide = g.astype(F32)
            ss[...] += jnp.sum((wide * wide).reshape(rows // 8, 8, 128), 0)

            @pl.when(c < chunks - slots)
            def _():
                for i, to in enumerate((partner, right, left)):
                    pl.semaphore_signal(free.at[i], inc=1, device_id={"dp": to}, device_id_type=pl.DeviceIdType.MESH)
        return 0

    lax.fori_loop(0, SEND[-1] + 1 + L3, step, 0)
    for c in (chunks - 2, chunks - 1):
        keep(c).wait()
    tell = [remote(ss, ssr.at[o], x_s.at[o], x_r.at[o], lax.rem(me + o, n)) for o in range(1, n)]
    for one in tell:
        one.start()
    total = ss[...]
    for o, one in enumerate(tell, 1):
        one.wait()
        total = total + ssr[o]
    ss_ref[...] = total

def grads(n, s, gu, at, h, dy, wg, wu, wd):
    t, d = h.shape
    ff = wg.shape[2]
    chunks, rows = 6 * NK, ff // NK // 128 * (d // n)
    assert rows == d // 128 * (ff // n // NK)
    half, slots, dma = rows // 2, chunks // 2, pltpu.SemaphoreType.DMA
    hbm = lambda a: pltpu.with_memory_space_constraint(a, pltpu.HBM)
    return pl.pallas_call(
        functools.partial(grads_kernel, n),
        in_specs=[pl.BlockSpec(memory_space=pltpu.HBM)] * 8,
        out_specs=[pl.BlockSpec(memory_space=pltpu.HBM), pl.BlockSpec(memory_space=pltpu.VMEM)],
        out_shape=[pltpu.HBM((chunks, rows, 128), BF16), pltpu.VMEM((8, 128), F32)],
        scratch_shapes=[pltpu.VMEM((d, t), BF16), pltpu.VMEM((t, d), BF16), pltpu.VMEM((2, t, ff // NK), BF16),
                        pltpu.VMEM((2, d, ff), BF16), pltpu.VMEM((ff // NK, d), BF16), pltpu.VMEM((2, 2, t // 4, ff // NK), F32),
                        pltpu.VMEM((t // 4, d), BF16), pltpu.VMEM((2, rows, 128), BF16),
                        pltpu.VMEM((RING + AHEAD, n // 2, rows, 128), BF16), pltpu.VMEM((slots, n // 2, rows, 128), BF16),
                        pltpu.VMEM((PENDING, 4, half, 128), BF16), pltpu.VMEM((slots, 2, half, 128), BF16),
                        pltpu.VMEM((PENDING, 2, half, 128), BF16), pltpu.VMEM((slots, 2, rows, 128), BF16),
                        pltpu.VMEM((8, 128), F32), pltpu.VMEM((n, 8, 128), F32),
                        dma((2,)), dma((3,)), dma((2, 2)), dma((3, 3)), dma((2,)), dma((PENDING,)), dma((chunks,)), dma((PENDING, 4)), dma((chunks, 4)),
                        dma((PENDING, 2)), dma((chunks, 2)), dma((n,)), dma((n,)), pltpu.SemaphoreType.REGULAR((3,))],
        compiler_params=pltpu.CompilerParams(vmem_limit_bytes=60 << 20, collective_id=0, has_side_effects=True),
        name="grads",
    )(*(hbm(a) for a in (s, gu, at, h, dy, wg, wu, wd)))


def update_kernel(n, count, ss_ref, g_hbm, *refs):
    given, outs, (g_ref, in_sem, g_sem, s_sem, r_sem) = refs[:9], refs[9:18], refs[18:]
    me = lax.axis_index("dp")
    chips = n // 2
    core, chip = lax.rem(me, 2), lax.div(me, 2)
    owner = lambda c, q=None: lax.rem(c + chips, chips) * 2 + (core if q is None else q)
    right, left, partner = owner(chip + 1), owner(chip - 1), owner(chip, 1 - core)
    pieces = [(i, l) for i in range(3) for l in range(2)]

    def rows_of(i, b, k=0, part=1):
        rows = outs[3 + i].shape[1]
        return pl.ds(pl.multiple_of(b * rows + k * (rows // part), 16), rows // part)

    def place(i, l, b):
        return outs[i].at[l, rows_of(i, b), :]

    def chunk_of(i, l, k):
        return i * NK + k if l else 3 * NK + k if i == 2 else 4 * NK + 2 * k + i

    def arrive(p):
        i, l = pieces[p]
        return (pltpu.make_async_copy(given[i].at[l, rows_of(i, me), :], place(i, l, me), in_sem.at[0, p]),
                pltpu.make_async_copy(given[3 + i].at[l], outs[3 + i].at[l], in_sem.at[1, p]),
                pltpu.make_async_copy(given[6 + i].at[l], outs[6 + i].at[l], in_sem.at[2, p]),
                *(pltpu.make_async_copy(g_hbm.at[chunk_of(i, l, k)], g_ref.at[chunk_of(i, l, k)], g_sem.at[p, k]) for k in range(NK)))
    for p in range(2):
        for one in arrive(p):
            one.start()
    barrier = pltpu.get_barrier_semaphore()
    for to in (left, right, partner):
        pl.semaphore_signal(barrier, inc=1, device_id={"dp": to}, device_id_type=pl.DeviceIdType.MESH)
    total = jnp.sum(ss_ref[...], keepdims=True)
    factor = jnp.minimum(1.0, 0.5 * lax.rsqrt(total / count + 1e-30))

    def renew(p):
        i, l = pieces[p]
        for one in arrive(p):
            one.wait()
        if p + 2 < len(pieces):
            for one in arrive(p + 2):
                one.start()
        full, cols = outs[3 + i].shape[1:]
        rows, tiles = (full, cols // NK // 128) if i < 2 else (full // NK, cols // 128)

        def part(k, _):
            for t in range(tiles):
                if i < 2:
                    r, own = pl.ds(0, full), rows_of(i, me)
                    c = pl.ds(pl.multiple_of(k * (cols // NK) + t * 128, 128), 128)
                else:
                    r, own = pl.ds(pl.multiple_of(k * rows, 16), rows), rows_of(i, me, k, NK)
                    c = pl.ds(t * 128, 128)
                g = g_ref[chunk_of(i, l, k), t * rows:(t + 1) * rows, :].astype(F32) * factor
                m = 0.9 * outs[3 + i][l, r, c] + 0.1 * g
                v = 0.95 * outs[6 + i][l, r, c] + 0.05 * g * g
                w = outs[i][l, own, c].astype(F32)
                outs[i][l, own, c] = (w - 0.02 * (m * lax.rsqrt(v + 1e-8) + 0.1 * w)).astype(BF16)
                outs[3 + i][l, r, c] = m
                outs[6 + i][l, r, c] = v
            return 0
        lax.fori_loop(0, NK, part, 0)

    def copy(kind, p):
        i, l = pieces[p]
        if kind == 0:
            to, b = right, me
        elif kind == 1:
            to, b = left, me
        elif kind == 2:
            to, b = (right, owner(chip - 1)) if l == 0 else (left, owner(chip + 1))
        else:
            to = partner
            b = (me, owner(chip - 1), owner(chip + 1), owner(chip + 2))[kind - 3]
        ref = place(i, l, b)
        return pltpu.make_async_remote_copy(src_ref=ref, dst_ref=ref, send_sem=s_sem.at[kind, p], recv_sem=r_sem.at[kind, p],
                                            device_id={"dp": to}, device_id_type=pl.DeviceIdType.MESH)
    zero, one_ = [p for p, (i, l) in enumerate(pieces) if l == 0], [p for p, (i, l) in enumerate(pieces) if l == 1]
    for p in range(len(pieces)):
        renew(p)
        if p == 0:
            pl.semaphore_wait(barrier, 3)
        if p > 0:
            copy(0 if pieces[p - 1][1] == 0 else 1, p - 1).start()
    copy(1, len(pieces) - 1).start()
    for a, b in zip(zero, one_):
        copy(0, b).start()
        copy(1, a).start()
    for p in range(len(pieces)):
        copy(3, p).start()
    for a, b in zip(zero, one_):
        copy(0, a).wait_recv()
        copy(2, a).start()
        copy(4, a).start()
        copy(1, b).wait_recv()
        copy(2, b).start()
        copy(5, b).start()
    for a, b in zip(one_, zero):
        copy(0, a).wait_recv()
        copy(4, a).start()
        copy(1, b).wait_recv()
        copy(5, b).start()
    for a, b in zip(zero, one_):
        for p in (a, b):
            copy(2, p).wait_recv()
            copy(6, p).start()
    for p in range(len(pieces)):
        for kind in range(7):
            copy(kind, p).wait_send()
            if kind >= 3:
                copy(kind, p).wait_recv()

def update(n, ss, g, ws, ms, vs):
    dma, vmem = pltpu.SemaphoreType.DMA, pl.BlockSpec(memory_space=pltpu.VMEM)
    count = n * sum(m.size for m in ms)
    out = pl.pallas_call(
        functools.partial(update_kernel, n, count),
        in_specs=[vmem] + [pl.BlockSpec(memory_space=pltpu.HBM)] * 10,
        out_specs=[vmem] * 9,
        out_shape=[pltpu.VMEM(a.shape, a.dtype) for a in (*ws, *ms, *vs)],
        scratch_shapes=[pltpu.VMEM(g.shape, BF16), dma((3, 6)), dma((6, NK)), dma((7, 6)), dma((7, 6))],
        compiler_params=pltpu.CompilerParams(vmem_limit_bytes=8 << 20, collective_id=1, has_side_effects=True),
        name="update",
    )(ss, *(pltpu.with_memory_space_constraint(a, pltpu.HBM) for a in (g, *ws, *ms, *vs)))
    return out

def store_kernel(*refs):
    half = (len(refs) - 1) // 2
    copies = [pltpu.make_async_copy(refs[i], refs[half + i], refs[-1].at[i]) for i in range(half)]
    for one in copies:
        one.start()
    for one in copies:
        one.wait()

def store(arrays):
    k = len(arrays)
    return pl.pallas_call(
        store_kernel, in_specs=[pl.BlockSpec(memory_space=pltpu.VMEM)] * k, out_specs=[pl.BlockSpec(memory_space=pltpu.HBM)] * k,
        out_shape=[pltpu.HBM(a.shape, a.dtype) for a in arrays], scratch_shapes=[pltpu.SemaphoreType.DMA((k,))],
        compiler_params=pltpu.CompilerParams(vmem_limit_bytes=1 << 20), name="store")(*arrays)

def solution(mesh):
    n = mesh.shape["dp"]

    def step(x, dy, wg, wu, wd, mg, mu, md, vg, vu, vd):
        s, gu, at, h = tokens(x, dy, wg, wu, wd)
        g, ss = grads(n, s, gu, at, h, dy, wg, wu, wd)
        return tuple(store(update(n, ss, g, (wg, wu, wd), (mg, mu, md), (vg, vu, vd))))

    data, whole, rows = P(("rep", "dp"), None, None), P(None, None, None), P(None, "dp", None)
    return jax.shard_map(step, mesh=mesh, in_specs=(data,) * 2 + (whole,) * 3 + (rows,) * 6,
                         out_specs=(P("rep", None, None),) * 3 + (P("rep", "dp", None),) * 6, check_vma=False)
```

time: 361 us -> 352 us (0.975)
  Pallas kernels: 356 us -> 351 us
    pallas_call x1, Pallas kernels: 114 us -> 80.2 us  [tokens(): pl.pallas_call(functools.partial(tokens_kernel, nf), grid=(t // tm,), in_...]
    pallas_call x1, Pallas kernels: 121 us -> 149 us  [grads(): pl.pallas_call(functools.partial(grads_kernel, n), in_specs=[pl.BlockSpec...]
where the time goes in v4:
time: 352 us
  Pallas kernels  351 us (100%)
    pallas_call x1, Pallas kernels, grads(): pl.pallas_call(functools.partial(grads_kernel, n), in_specs=[pl.BlockSpec...  149 us
    pallas_call x1, Pallas kernels, update(): pl.pallas_call(functools.partial(update_kernel, n, count), in_specs=[vmem...  109 us
    pallas_call x1, Pallas kernels, tokens(): pl.pallas_call(functools.partial(tokens_kernel, nf), grid=(t // tm,), in_...  80.2 us
    pallas_call x1, Pallas kernels, store(): pl.pallas_call(store_kernel, in_specs=[pl.BlockSpec(memory_space=pltpu.VM...  12.2 us

profile of v4, /device:TPU:113, one launch (start us, length us, event | category | flops | bytes accessed | tf_op | source)
XLA Modules:
  0.0 351.9 jit_solution(16338975780306045787)
XLA Ops:
  0.6 80.2 %tokens.1 = (bf16[4,2048,2304]{2,1,0:T(8,128)(2,1)}, f32[2,2048,2304]{2,1,0:T(8,128)}, bf16[2,896,2048]{2,1,0:T(8,128)(2,1)}, bf16[2048,896]{1,0:T(8,128)(2,1)}) custom-call(bf16[1,2048,896]{2,1,0:T(8,128)(2,1)} %x_ref.1, bf16[1,2048,896]{2,1,0:T(8,128)(2,1)} %dy_hbm.1, bf16[2,896,2304]{2,1,0:T(8,128)(2,1)} %refs_0_.1, bf16[2,896,2304]{2,1,0:T(8,128)(2,1)} %refs_1_.1, ...), custom_call_target="tpu_custom_call" | custom-call | tf_op jit(solution)/shard_map/tokens/pallas_call | solution.py:82
  80.8 149.4 %grads.1 = (bf16[18,672,128]{2,1,0:T(8,128)(2,1)}, f32[8,128]{1,0:T(8,128)S(1)}) custom-call(bf16[4,2048,2304]{2,1,0:T(8,128)(2,1)} %get-tuple-element.24.s_hbm, f32[2,2048,2304]{2,1,0:T(8,128)} %get-tuple-element.25.gu_hbm, bf16[2,896,2048]{2,1,0:T(8,128)(2,1)} %get-tuple-element.26.at_hbm, bf16[2048,896]{1,0:T(8,128)(2,1)} %get-tuple-element.27.h_hbm, ...), custom_call_target="tpu_custom_call" | custom-call | tf_op jit(solution)/shard_map/grads/pallas_call | solution.py:403
  230.3 109.3 %update.1 = (bf16[2,896,2304]{2,1,0:T(8,128)(2,1)S(1)}, bf16[2,896,2304]{2,1,0:T(8,128)(2,1)S(1)}, bf16[2,2304,896]{2,1,0:T(8,128)(2,1)S(1)}, f32[2,112,2304]{2,...) custom-call(f32[8,128]{1,0:T(8,128)S(1)} %get-tuple-element.28.ss_re, ...), custom_call_target="tpu_custom_call" | custom-call | tf_op jit(solution)/shard_map/update/pallas_call | solution.py:536
  339.6 12.2 %store.1 = (bf16[2,896,2304]{2,1,0:T(8,128)(2,1)}, bf16[2,896,2304]{2,1,0:T(8,128)(2,1)}, bf16[2,2304,896]{2,1,0:T(8,128)(2,1)}, f32[2,112,2304]{2,1,0:T(8,128)}...) custom-call(bf16[2,896,2304]{2,1,0:T(8,128)(2,1)S(1)} %get-tuple-ele, ...), custom_call_target="tpu_custom_call" | custom-call | tf_op jit(solution)/shard_map/store/pallas_call | solution.py:557

commit v5 on v4

--- a/solution.py
+++ b/solution.py
@@ -92,7 +92,7 @@
 
 TN = (((0,), (0,)), ((), ()))
 NK, RING, AHEAD = 3, 9, 5
-L1, L2, L3 = 1, 3, 5
+L1, L2, L3 = 1, 3, 6
 WHEN = (*range(6), 5, 6, *range(6, 12), 11, *range(11, 18))
 SEND = (*range(9), 11, *range(11, 13), *range(12, 18))
 PENDING = 6

time: 352 us -> 352 us (level)
  no operation moved by 1% of the time
where the time goes in v5:
time: 352 us
  Pallas kernels  351 us (100%)
    pallas_call x1, Pallas kernels, grads(): pl.pallas_call(functools.partial(grads_kernel, n), in_specs=[pl.BlockSpec...  149 us
    pallas_call x1, Pallas kernels, update(): pl.pallas_call(functools.partial(update_kernel, n, count), in_specs=[vmem...  109 us
    pallas_call x1, Pallas kernels, tokens(): pl.pallas_call(functools.partial(tokens_kernel, nf), grid=(t // tm,), in_...  80.2 us
    pallas_call x1, Pallas kernels, store(): pl.pallas_call(store_kernel, in_specs=[pl.BlockSpec(memory_space=pltpu.VM...  12.2 us

profile of v5, /device:TPU:113, one launch (start us, length us, event | category | flops | bytes accessed | tf_op | source)
XLA Modules:
  0.0 351.6 jit_solution(11694316324189037441)
XLA Ops:
  0.6 80.2 %tokens.1 = (bf16[4,2048,2304]{2,1,0:T(8,128)(2,1)}, f32[2,2048,2304]{2,1,0:T(8,128)}, bf16[2,896,2048]{2,1,0:T(8,128)(2,1)}, bf16[2048,896]{1,0:T(8,128)(2,1)}) custom-call(bf16[1,2048,896]{2,1,0:T(8,128)(2,1)} %x_ref.1, bf16[1,2048,896]{2,1,0:T(8,128)(2,1)} %dy_hbm.1, bf16[2,896,2304]{2,1,0:T(8,128)(2,1)} %refs_0_.1, bf16[2,896,2304]{2,1,0:T(8,128)(2,1)} %refs_1_.1, ...), custom_call_target="tpu_custom_call" | custom-call | tf_op jit(solution)/shard_map/tokens/pallas_call | solution.py:82
  80.8 149.1 %grads.1 = (bf16[18,672,128]{2,1,0:T(8,128)(2,1)}, f32[8,128]{1,0:T(8,128)S(1)}) custom-call(bf16[4,2048,2304]{2,1,0:T(8,128)(2,1)} %get-tuple-element.24.s_hbm, f32[2,2048,2304]{2,1,0:T(8,128)} %get-tuple-element.25.gu_hbm, bf16[2,896,2048]{2,1,0:T(8,128)(2,1)} %get-tuple-element.26.at_hbm, bf16[2048,896]{1,0:T(8,128)(2,1)} %get-tuple-element.27.h_hbm, ...), custom_call_target="tpu_custom_call" | custom-call | tf_op jit(solution)/shard_map/grads/pallas_call | solution.py:403
  230.0 109.3 %update.1 = (bf16[2,896,2304]{2,1,0:T(8,128)(2,1)S(1)}, bf16[2,896,2304]{2,1,0:T(8,128)(2,1)S(1)}, bf16[2,2304,896]{2,1,0:T(8,128)(2,1)S(1)}, f32[2,112,2304]{2,...) custom-call(f32[8,128]{1,0:T(8,128)S(1)} %get-tuple-element.28.ss_re, ...), custom_call_target="tpu_custom_call" | custom-call | tf_op jit(solution)/shard_map/update/pallas_call | solution.py:536
  339.3 12.2 %store.1 = (bf16[2,896,2304]{2,1,0:T(8,128)(2,1)}, bf16[2,896,2304]{2,1,0:T(8,128)(2,1)}, bf16[2,2304,896]{2,1,0:T(8,128)(2,1)}, f32[2,112,2304]{2,1,0:T(8,128)}...) custom-call(bf16[2,896,2304]{2,1,0:T(8,128)(2,1)S(1)} %get-tuple-ele, ...), custom_call_target="tpu_custom_call" | custom-call | tf_op jit(solution)/shard_map/store/pallas_call | solution.py:557
